TPU v7x, 32 devices: a whole 2x2x4 slice. The times are simulated.
32 devices in a mesh: tgt: 8 (over z, y), src: 2 (over x), grp: 2 (over core).
Axes of the slice: x: 2, y: 2, z: 4, core: 2. Of those that a mesh axis runs over, the one named last changes fastest.
Arguments:
- positions: float32 [3, 2048], P(None, ('tgt', 'src', 'grp')), may hold values from 0 to 1
- strengths: float32 [3, 2048], P(None, ('tgt', 'src', 'grp')), may hold values from -0.02 to 0.02
- live_counts: int32 [32], P(('tgt', 'src', 'grp')), may hold values from 1 to 64, 1280 in all
- vorticity: float32 [3, 96, 96, 256], P(None, 'tgt', ('src', 'grp')), may hold values from -6 to 6
- diffusivity: float32 [96, 96, 256], P('tgt', ('src', 'grp')), may hold values from 0.02 to 0.15
- seed_counts: int32 [96, 96, 256], P('tgt', ('src', 'grp')), may hold values from 0 to 7
Outputs:
- vorticity_next: float32 [3, 96, 96, 256], P(None, 'tgt', ('src', 'grp'))
- particle_rates: float32 [6, 2048], P(None, ('tgt', 'src', 'grp'))
- blob_velocity: float32 [3, 4096], P(None, ('tgt', 'src', 'grp'))
Inputs may be any that keep to these rules, and one draw needn't show every extreme that they name: `live_counts`: the values sum to 32 * 64 * 5 // 8.
All inputs are finite; a program needn't handle non-finite values.
Results may differ from a plain program's by a relative error of at most 0.000095.
Values sent between devices are 32-bit elements; how exact they have to be, the bound alone decides.
No kernel may reach another device: no remote copies, remote signals or barrier semaphores. Data moves between devices by JAX's collectives and lax.ppermute only.
A program may use at most 64 MiB of HBM per device.

v0:
```python
import functools
import jax
import jax.numpy as jnp
from jax import lax
from jax.experimental import pallas as pl
from jax.experimental.pallas import tpu as pltpu
from jax.sharding import PartitionSpec as P

BZ = 2
LANES = 128
GROUPS = 9

sigma_sq = 0.0004
kernel_scale = 0.25 / 3.141592653589793
seed_weight = 0.0001


VMEM = pl.BlockSpec(memory_space=pltpu.VMEM)
SMEM = pl.BlockSpec(memory_space=pltpu.SMEM)


def split3(value):
    high = value.astype(jnp.bfloat16)
    rest = value - high.astype(jnp.float32)
    middle = rest.astype(jnp.bfloat16)
    low = (rest - middle.astype(jnp.float32)).astype(jnp.bfloat16)
    return high, middle, low


def pair_lanes(rows):
    length = rows.shape[1]
    cell = lax.broadcasted_iota(jnp.int32, (length, length // BZ), 0)
    blob = lax.broadcasted_iota(jnp.int32, (length, length // BZ), 1)
    chosen = jnp.where((cell >= blob * BZ) & (cell < blob * BZ + BZ), 1.0, 0.0).astype(jnp.bfloat16)
    total = None
    for part in split3(rows):
        product = jnp.dot(part, chosen, preferred_element_type=jnp.float32)
        total = product if total is None else total + product
    return total


def shifted_rows(value, step):
    rows = lax.broadcasted_iota(jnp.int32, value.shape, 0)
    count = value.shape[0]
    if step == 1:
        return jnp.where(rows == 0, 0.0, pltpu.roll(value, 1, 0))
    return jnp.where(rows == count - 1, 0.0, pltpu.roll(value, count - 1, 0))


def shifted_lanes(value, step):
    lanes = lax.broadcasted_iota(jnp.int32, value.shape, 1)
    count = value.shape[1]
    if step == 1:
        return jnp.where(lanes == 0, 0.0, pltpu.roll(value, 1, 1))
    return jnp.where(lanes == count - 1, 0.0, pltpu.roll(value, count - 1, 1))


def here():
    x_index = lax.axis_index("tgt")
    y_index = lax.axis_index("src") * lax.axis_size("grp") + lax.axis_index("grp")
    return x_index, y_index


def faces_kernel(v_ref, xa_ref, xb_ref, ya_ref, yb_ref, low_ref, high_ref, sems):
    _, cells_x, cells_y, _ = v_ref.shape
    x_index, y_index = here()
    x_even = lax.rem(x_index, 2) == 0
    y_even = lax.rem(y_index, 2) == 0
    top = (cells_y - 1) // 8 * 8
    last = cells_x - 1
    copies = [
        pltpu.make_async_copy(v_ref.at[:, jnp.where(x_even, 0, last)], xb_ref, sems.at[0]),
        pltpu.make_async_copy(v_ref.at[:, jnp.where(x_even, last, 0)], xa_ref, sems.at[1]),
        pltpu.make_async_copy(v_ref.at[:, :, 0:8], low_ref, sems.at[2]),
        pltpu.make_async_copy(v_ref.at[:, :, top : top + 8], high_ref, sems.at[3]),
    ]
    for copy in copies:
        copy.start()
    copies[2].wait()
    copies[3].wait()
    for k in range(3):
        first = low_ref[k, :, 0, :]
        final = high_ref[k, :, cells_y - 1 - top, :]
        ya_ref[k] = jnp.where(y_even, final, first)
        yb_ref[k] = jnp.where(y_even, first, final)
    copies[0].wait()
    copies[1].wait()


def local_kernel(live_ref, v_ref, d_ref, c_ref, position_ref, strength_ref, sums_ref, wx_ref, wy_ref, row_ref):
    _, cells_x, cells_y, cells_z = v_ref.shape
    slot_count = position_ref.shape[1]
    w = []
    c = []
    for x in range(cells_x):
        counts = c_ref[x].astype(jnp.float32)
        c.append(counts)
        w.append(counts * d_ref[x])
    wx_ref[0] = w[0]
    wx_ref[1] = w[cells_x - 1]
    for x in range(cells_x):
        wy_ref[0, x : x + 1, :] = w[x][0:1, :]
        wy_ref[1, x : x + 1, :] = w[x][cells_y - 1 : cells_y, :]
    zero = jnp.zeros((cells_y, cells_z), jnp.float32)
    at = [zero] * 3
    after = [zero] * 3
    before = [zero] * 3
    plain = zero
    moment = zero
    for x in range(cells_x):
        beside = shifted_rows(w[x], 1) + shifted_rows(w[x], -1)
        if x > 0:
            beside = beside + w[x - 1]
        if x < cells_x - 1:
            beside = beside + w[x + 1]
        around = c[x] + (beside - 6.0 * w[x])
        up = shifted_lanes(w[x], 1)
        down = shifted_lanes(w[x], -1)
        for k in range(3):
            v = v_ref[k, x]
            at[k] = at[k] + around * v
            after[k] = after[k] + up * v
            before[k] = before[k] + down * v
        plain = plain + (c[x] + 1.0)
        moment = moment + (c[x] + 1.0) * (x + 0.5)
    rows = []
    for k in range(3):
        total = (
            jnp.sum(at[k], axis=0, keepdims=True)
            + shifted_lanes(jnp.sum(after[k], axis=0, keepdims=True), -1)
            + shifted_lanes(jnp.sum(before[k], axis=0, keepdims=True), 1)
        )
        rows.append(total)
    sums_ref[0:3, :] = jnp.concatenate(rows, axis=0)
    sums_ref[3:8, :] = jnp.zeros((5, cells_z), jnp.float32)
    y_centre = lax.broadcasted_iota(jnp.int32, (cells_y, cells_z), 0).astype(jnp.float32) + 0.5
    z_centre = lax.broadcasted_iota(jnp.int32, (1, cells_z), 1).astype(jnp.float32) + 0.5
    weight = jnp.sum(plain, axis=0, keepdims=True)
    moments = jnp.concatenate(
        [
            weight,
            jnp.sum(moment, axis=0, keepdims=True),
            jnp.sum(plain * y_centre, axis=0, keepdims=True),
            weight * z_centre,
            jnp.zeros((4, cells_z), jnp.float32),
        ],
        axis=0,
    )
    blobs = pair_lanes(moments)
    inverse = 1.0 / blobs[0:1]
    x_index, y_index = here()
    x_anchor = (x_index * cells_x).astype(jnp.float32)
    y_anchor = (y_index * cells_y).astype(jnp.float32)
    row_ref[0:1, :] = (blobs[1:2] * inverse + x_anchor) / cells_z
    row_ref[1:2, :] = (blobs[2:3] * inverse + y_anchor) / cells_z
    row_ref[2:3, :] = (blobs[3:4] * inverse) / cells_z
    alive = lax.broadcasted_iota(jnp.int32, (3, slot_count), 1) < live_ref[0]
    strength = jnp.where(alive, strength_ref[...], 0.0)
    parts = [position_ref[k : k + 1] for k in range(3)] + [strength[k : k + 1] for k in range(3)]
    for k in range(3):
        row_ref[3 + k : 4 + k, :] = jnp.concatenate(parts[2 * k : 2 * k + 2], axis=1)


def block_kernel(sums_ref, wx_ref, wy_ref, row_ref, xa_ref, xb_ref, ya_ref, yb_ref, out_ref, own_ref):
    x_index, y_index = here()
    x_even = lax.rem(x_index, 2) == 0
    y_even = lax.rem(y_index, 2) == 0
    total = sums_ref[...]
    rows = []
    for k in range(3):
        first = jnp.where(x_even, xb_ref[k], xa_ref[k])
        last = jnp.where(x_even, xa_ref[k], xb_ref[k])
        row = jnp.sum(wx_ref[0] * first + wx_ref[1] * last, axis=0, keepdims=True)
        first = jnp.where(y_even, yb_ref[k], ya_ref[k])
        last = jnp.where(y_even, ya_ref[k], yb_ref[k])
        row = row + jnp.sum(wy_ref[0] * first + wy_ref[1] * last, axis=0, keepdims=True)
        rows.append(row)
    total = total + jnp.concatenate(rows + [jnp.zeros((5, total.shape[1]), jnp.float32)], axis=0)
    strength = seed_weight * pair_lanes(total)
    block = jnp.concatenate([row_ref[0:3], strength[0:3], row_ref[3:6]], axis=0)
    own_ref[0:GROUPS, :] = block
    devices = out_ref.shape[0] // GROUPS
    for device in range(devices):
        out_ref[device * GROUPS : (device + 1) * GROUPS, :] = block


def target_rows(own):
    rows = []
    for k in range(3):
        row = own[6 + k : 7 + k]
        rows.append(row)
        rows.append(pltpu.roll(row, LANES // 2, 1))
    return rows


def grid_kernel(v_ref, d_ref, xa_ref, xb_ref, ya_ref, yb_ref, own_ref, out_ref, column_ref):
    _, cells_x, cells_y, cells_z = v_ref.shape
    x_index, y_index = here()
    x_even = lax.rem(x_index, 2) == 0
    y_even = lax.rem(y_index, 2) == 0
    rows = lax.broadcasted_iota(jnp.int32, (cells_y, cells_z), 0)
    for k in range(3):
        before = jnp.where(x_even, xb_ref[k], xa_ref[k])
        beyond = jnp.where(x_even, xa_ref[k], xb_ref[k])
        first = jnp.where(y_even, yb_ref[k], ya_ref[k])
        last = jnp.where(y_even, ya_ref[k], yb_ref[k])
        for x in range(cells_x):
            v = v_ref[k, x]
            low = before if x == 0 else v_ref[k, x - 1]
            high = beyond if x == cells_x - 1 else v_ref[k, x + 1]
            left = jnp.where(rows == 0, first[x : x + 1], pltpu.roll(v, 1, 0))
            right = jnp.where(rows == cells_y - 1, last[x : x + 1], pltpu.roll(v, cells_y - 1, 0))
            beside = (high + low) + (right + left) + (shifted_lanes(v, -1) + shifted_lanes(v, 1))
            out_ref[k, x] = v + d_ref[x] * (beside - 6.0 * v)

    own = own_ref[0:GROUPS, :]
    particles = target_rows(own)
    zeros = jnp.zeros((1, LANES), jnp.float32)
    wide = [jnp.concatenate([own[k : k + 1], particles[k]], axis=1) for k in range(3)]
    wide = wide + [jnp.concatenate([zeros, particles[k]], axis=1) for k in range(3, 6)]
    table = jnp.concatenate(wide + [jnp.zeros((LANES - 6, 2 * LANES), jnp.float32)], axis=0)
    columns = jnp.transpose(table)
    targets = column_ref.shape[1]
    for k in range(6):
        begin = 0 if k < 3 else LANES
        column_ref[k, begin:targets, :] = jnp.broadcast_to(columns[begin:targets, k : k + 1], (targets - begin, LANES))


def pair_kernel(live_ref, all_ref, own_ref, column_ref, rates_ref, blob_ref, source_ref, feature_ref, turn_ref, sum_ref, *, cells):
    devices = all_ref.shape[0] // GROUPS
    half = LANES // 2
    tiles = devices + devices // 2
    targets = column_ref.shape[1]
    lane = lax.broadcasted_iota(jnp.int32, (devices, LANES), 1)
    x_index, y_index = here()
    centre = [
        (x_index.astype(jnp.float32) + 0.5) * (cells[0] / cells[2]),
        (y_index.astype(jnp.float32) + 0.5) * (cells[1] / cells[2]),
        0.5,
    ]

    def group(index):
        return all_ref[pl.ds(index, devices, stride=GROUPS), :]

    def evens(rows):
        turn_ref[...] = rows
        return turn_ref[pl.ds(0, devices // 2, stride=2), :]

    blobs = [group(k) for k in range(6)]
    particles = []
    for k in range(3):
        both = group(6 + k)
        turned = pltpu.roll(both, half, 1)
        particles.append(evens(jnp.where(lane < half, both, pltpu.roll(turned, devices - 1, 0))))
        particles.append(evens(jnp.where(lane < half, turned, pltpu.roll(both, devices - 1, 0))))
    elements = [jnp.concatenate([blobs[k], particles[k]], axis=0) for k in range(6)]
    for k in range(3):
        source_ref[k * tiles : (k + 1) * tiles, :] = elements[k]
    place = [elements[k] - centre[k] for k in range(3)]
    a = elements[3:]
    features = a + [
        place[1] * a[2] - place[2] * a[1],
        place[2] * a[0] - place[0] * a[2],
        place[0] * a[1] - place[1] * a[0],
    ]
    feature_ref[...] = jnp.zeros_like(feature_ref)
    for k in range(6):
        parts = split3(features[k])
        for j in range(3):
            row = (8 * j + k) * tiles
            feature_ref[row : row + tiles, :] = parts[j].astype(jnp.float32)

    sum_ref[...] = jnp.zeros_like(sum_ref)
    block = 32
    width = 4 if tiles % 4 == 0 else 1
    steps = tiles // width
    unroll = next(n for n in (12, 8, 6, 4, 3, 2, 1) if steps % n == 0)
    contract = (((1,), (1,)), ((), ()))

    def product(values, feature):
        highs = [value.astype(jnp.bfloat16) for value in values]
        lows = [(value - high.astype(jnp.float32)).astype(jnp.bfloat16) for value, high in zip(values, highs)]
        both = jnp.concatenate([jnp.concatenate(highs, axis=1), jnp.concatenate(lows, axis=1)], axis=0)
        return lax.dot_general(both, feature, contract, preferred_element_type=jnp.float32)

    def one(chunk):
        spans = [chunk * width + j for j in range(width)]
        feature = jnp.concatenate([feature_ref[pl.ds(tile, 32, stride=tiles), :].astype(jnp.bfloat16) for tile in spans], axis=1)
        source = [[source_ref[pl.ds(k * tiles + tile, 1), :] for k in range(3)] for tile in spans]
        for t in range(0, targets, block):
            kernels, pulls = [], []
            for j in range(width):
                sep = [column_ref[k, t : t + block, :] - source[j][k] for k in range(3)]
                squared = sep[0] * sep[0] + sep[1] * sep[1] + (sep[2] * sep[2] + sigma_sq)
                inverse = lax.rsqrt(squared)
                square = inverse * inverse
                kernel = square * inverse
                kernels.append(kernel)
                if t >= LANES:
                    along = column_ref[3, t : t + block, :] * sep[0] + column_ref[4, t : t + block, :] * sep[1] + column_ref[5, t : t + block, :] * sep[2]
                    pulls.append((kernel * square) * along)
            rows = slice(2 * t, 2 * t + 2 * block)
            sum_ref[rows, 0:32] = sum_ref[rows, 0:32] + product(kernels, feature)
            if t >= LANES:
                rows = slice(2 * (targets + t - LANES), 2 * (targets + t - LANES) + 2 * block)
                sum_ref[rows, 0:32] = sum_ref[rows, 0:32] + product(pulls, feature)

    def step(index, _):
        for j in range(unroll):
            one(index * unroll + j)
        return 0

    lax.fori_loop(0, steps // unroll, step, 0)

    def combined(begin, end):
        parts = [sum_ref[2 * t : 2 * t + block] + sum_ref[2 * t + block : 2 * t + 2 * block] for t in range(begin, end, block)]
        rest = -(end - begin) % LANES
        if rest:
            parts.append(jnp.zeros((rest, LANES), jnp.float32))
        turned = jnp.transpose(jnp.concatenate(parts, axis=0))
        return turned[0:8] + turned[8:16] + turned[16:24]

    found = combined(0, targets)
    pulled = combined(targets, targets + half)

    def crossed(place, rows):
        return [
            place[1] * rows[2:3] - place[2] * rows[1:2] - rows[3:4],
            place[2] * rows[0:1] - place[0] * rows[2:3] - rows[4:5],
            place[0] * rows[1:2] - place[1] * rows[0:1] - rows[5:6],
        ]

    own = own_ref[0:GROUPS, :]
    slots = target_rows(own)
    near = found[:, LANES:]
    alive = (lax.broadcasted_iota(jnp.int32, (1, LANES), 1) < live_ref[0]).astype(jnp.float32)
    blob_place = [own[k : k + 1] - centre[k] for k in range(3)]
    slot_place = [slots[k] - centre[k] for k in range(3)]
    a = slots[3:]
    first = [
        a[1] * near[2:3] - a[2] * near[1:2],
        a[2] * near[0:1] - a[0] * near[2:3],
        a[0] * near[1:2] - a[1] * near[0:1],
    ]
    blob_velocity = crossed(blob_place, found[:, 0:LANES])
    slot_velocity = crossed(slot_place, near)
    second = crossed(slot_place, pulled)
    for k in range(3):
        blob_ref[k : k + 1, :] = -kernel_scale * blob_velocity[k]
        rates_ref[k : k + 1, :] = (-kernel_scale * slot_velocity[k] * alive)[:, 0:half]
        rates_ref[3 + k : 4 + k, :] = (-kernel_scale * (first[k] - 3.0 * second[k]) * alive)[:, 0:half]


def partners(count, start):
    pairs = [(i, i + 1) for i in range(start, count - 1, 2)]
    return pairs + [(j, i) for i, j in pairs]


def per_device(positions, strengths, live_counts, vorticity, diffusivity, seed_counts):
    _, cells_x, cells_y, cells_z = vorticity.shape
    slot_count = positions.shape[1]
    y_axes = ("src", "grp")
    everyone = ("tgt", "src", "grp")
    x_count, y_count = lax.axis_size("tgt"), lax.axis_size("src") * lax.axis_size("grp")
    devices = x_count * y_count
    f32 = jnp.float32

    def kept(*shape):
        return pltpu.VMEM(shape, f32)

    def held(array):
        return pltpu.with_memory_space_constraint(array, pltpu.VMEM)

    xa, xb, ya, yb = pl.pallas_call(
        faces_kernel,
        name="faces",
        out_shape=(kept(3, cells_y, cells_z), kept(3, cells_y, cells_z), kept(3, cells_x, cells_z), kept(3, cells_x, cells_z)),
        in_specs=[pl.BlockSpec(memory_space=pl.ANY)],
        out_specs=[VMEM] * 4,
        scratch_shapes=[
            pltpu.VMEM((3, cells_x, 8, cells_z), f32),
            pltpu.VMEM((3, cells_x, 8, cells_z), f32),
            pltpu.SemaphoreType.DMA((4,)),
        ],
    )(vorticity)
    xa = held(lax.ppermute(xa, "tgt", partners(x_count, 0)))
    xb = held(lax.ppermute(xb, "tgt", partners(x_count, 1)))
    ya = held(lax.ppermute(ya, y_axes, partners(y_count, 0)))
    yb = held(lax.ppermute(yb, y_axes, partners(y_count, 1)))

    v, d, c = held(vorticity), diffusivity, seed_counts
    sums, wx, wy, rows = pl.pallas_call(
        local_kernel,
        name="local",
        out_shape=(kept(8, cells_z), kept(2, cells_y, cells_z), kept(2, cells_x, cells_z), kept(8, LANES)),
        in_specs=[SMEM] + [VMEM] * 5,
        out_specs=[VMEM] * 4,
    )(live_counts, v, d, c, positions, strengths)
    block, own = pl.pallas_call(
        block_kernel,
        name="block",
        out_shape=(jax.ShapeDtypeStruct((devices * GROUPS, LANES), f32), kept(16, LANES)),
        in_specs=[VMEM] * 8,
        out_specs=[VMEM] * 2,
    )(held(sums), held(wx), held(wy), held(rows), xa, xb, ya, yb)
    everything = lax.all_to_all(block.reshape(-1), everyone, 0, 0, tiled=True).reshape(devices * GROUPS, LANES)

    targets = LANES + slot_count
    vorticity_next, columns = pl.pallas_call(
        grid_kernel,
        name="grid",
        out_shape=(jax.ShapeDtypeStruct(vorticity.shape, f32), kept(6, targets, LANES)),
        in_specs=[VMEM] * 7,
        out_specs=[VMEM] * 2,
    )(v, d, xa, xb, ya, yb, held(own))

    tiles = devices + devices // 2
    particle_rates, blob_velocity = pl.pallas_call(
        functools.partial(pair_kernel, cells=(cells_x, cells_y, cells_z)),
        name="pairs",
        out_shape=(jax.ShapeDtypeStruct((6, slot_count), f32), jax.ShapeDtypeStruct((3, LANES), f32)),
        in_specs=[SMEM] + [VMEM] * 3,
        out_specs=[VMEM, VMEM],
        scratch_shapes=[
            pltpu.VMEM((3 * tiles, LANES), f32),
            pltpu.VMEM((32 * tiles, LANES), f32),
            pltpu.VMEM((devices, LANES), f32),
            pltpu.VMEM((2 * targets + 2 * slot_count, LANES), f32),
        ],
    )(live_counts, held(everything), held(own), held(columns))
    return (vorticity_next, particle_rates, blob_velocity)


def solution(mesh):
    placed = (
        P(None, ("tgt", "src", "grp")),
        P(None, ("tgt", "src", "grp")),
        P(("tgt", "src", "grp")),
        P(None, "tgt", ("src", "grp"), None),
        P("tgt", ("src", "grp"), None),
        P("tgt", ("src", "grp"), None),
    )
    return jax.shard_map(
        per_device,
        mesh=mesh,
        in_specs=placed,
        out_specs=(
            P(None, "tgt", ("src", "grp"), None),
            P(None, ("tgt", "src", "grp")),
            P(None, ("tgt", "src", "grp")),
        ),
        check_vma=False,
    )
```

profile of v0, /device:TPU:0, one launch (start us, length us, event | category | flops | bytes accessed | tf_op | source)
XLA Modules:
  0.0 32.7 jit_solution(17686347418543830929)
XLA Ops:
  0.6 0.0 copy-start
  0.6 1.3 %faces.1 = (f32[3,24,256]{2,1,0:T(8,128)S(1)}, f32[3,24,256]{2,1,0:T(8,128)S(1)}, f32[3,12,256]{2,1,0:T(8,128)S(1)}, f32[3,12,256]{2,1,0:T(8,128)S(1)}) custom-call(f32[3,12,24,256]{3,2,1,0:T(8,128)} %v_ref.5), custom_call_target="tpu_custom_call" | custom-call | tf_op jit(solution)/shard_map/faces/pallas_call | solution.py:374
  1.9 3.1 %collective-permute-start = (f32[3,24,256]{2,1,0:T(8,128)S(1)}, f32[3,24,256]{2,1,0:T(8,128)S(1)}, u32[]{:S(2)}, u32[]{:S(2)}) collective-permute-start(f32[3,24,256]{2,1,0:T(8,128)S(1)} %get-tuple-element.17), channel_id=1, source_target_pairs={{0,4},{8,12},{16,20},{24,28},{4,0},{12,8},{20,16},{28,24},{1,5},{9... | collective-permute-start | bytes 221192 | tf_op jit(solution)/shard_map/ppermute | solution.py:386
  5.0 0.7 %collective-permute-start.1 = (f32[3,24,256]{2,1,0:T(8,128)S(1)}, f32[3,24,256]{2,1,0:T(8,128)S(1)}, u32[]{:S(2)}, u32[]{:S(2)}) collective-permute-start(f32[3,24,256]{2,1,0:T(8,128)S(1)} %get-tuple-element.18), channel_id=1, source_target_pairs={{4,8},{12,16},{20,24},{8,4},{16,12},{24,20},{5,9},{13,17},{21,25},... | collective-permute-start | bytes 221192 | tf_op jit(solution)/shard_map/ppermute | solution.py:387
  5.7 0.1 collective-permute-start.2
  5.7 0.7 %collective-permute-start.3 = (f32[3,12,256]{2,1,0:T(8,128)S(1)}, f32[3,12,256]{2,1,0:T(8,128)S(1)}, u32[]{:S(2)}, u32[]{:S(2)}) collective-permute-start(f32[3,12,256]{2,1,0:T(8,128)S(1)} %get-tuple-element.20), channel_id=1, source_target_pairs={{1,2},{2,1},{5,6},{6,5},{9,10},{10,9},{13,14},{14,13},{17,18},{18,... | collective-permute-start | bytes 110600 | tf_op jit(solution)/shard_map/ppermute | solution.py:389
  7.1 0.0 copy-done
  7.1 1.6 %local.1 = (f32[8,256]{1,0:T(8,128)S(1)}, f32[2,24,256]{2,1,0:T(8,128)S(1)}, f32[2,12,256]{2,1,0:T(8,128)S(1)}, f32[8,128]{1,0:T(8,128)S(1)}) custom-call(s32[1]{0:T(128)S(6)} %copy.10.live_ref, f32[3,12,24,256]{3,2,1,0:T(8,128)S(1)} %copy-done, f32[12,24,256]{2,1,0:T(8,128)} %d_ref.3, s32[12,24,256]{2,1,0:T(8,128)} %c_ref.1, f32[3,64]{1,0:T(4,128)} %position_ref.1, ...), custom_call_target="tpu_custom_call" | custom-call | tf_op jit(solution)/shard_map/local/pallas_call | solution.py:392
  8.7 0.0 collective-permute-done.2.ya_ref
  8.7 0.0 collective-permute-done.3.yb_ref
  8.7 0.0 collective-permute-done.xa_ref
  8.7 0.0 collective-permute-done.1.xb_ref
  8.7 0.9 %block.1 = (f32[288,128]{1,0:T(8,128)}, f32[16,128]{1,0:T(8,128)S(1)}) custom-call(f32[8,256]{1,0:T(8,128)S(1)} %get-tuple-element.21.sums_ref, f32[2,24,256]{2,1,0:T(8,128)S(1)} %get-tuple-element.22.wx_ref, f32[2,12,256]{2,1,0:T(8,128)S(1)} %get-tuple-element.23.wy_ref, f32[8,128]{1,0:T(8,128)S(1)} %get-tuple-element.24.row_ref, ...), custom_call_target="tpu_custom_call" | custom-call | tf_op jit(solution)/shard_map/block/pallas_call | solution.py:399
  9.6 10.1 %all-to-all-start = ((f32[32,1152,1]{1,2,0:T(1,128)}), f32[32,1152,1]{1,2,0:T(1,128)S(1)}, u32[]{:S(2)}, u32[]{:S(2)}) async-start(f32[32,1152,1]{1,2,0:T(1,128)} %bitcast.3), calls=%async_computation | async-start | bytes 294912 | tf_op jit(solution)/shard_map/all_to_all | solution.py:406
  19.6 2.5 %grid.1 = (f32[3,12,24,256]{3,2,1,0:T(8,128)}, f32[6,192,128]{2,1,0:T(8,128)S(1)}) custom-call(f32[3,12,24,256]{3,2,1,0:T(8,128)S(1)} %copy-done, f32[12,24,256]{2,1,0:T(8,128)} %d_ref.3, f32[3,24,256]{2,1,0:T(8,128)S(1)} %collective-permute-done.xa_ref, f32[3,24,256]{2,1,0:T(8,128)S(1)} %collective-permute-done.1.xb_ref, ...), custom_call_target="tpu_custom_call" | custom-call | tf_op jit(solution)/shard_map/grid/pallas_call | solution.py:409
  22.2 5.9 %all-to-all-done = f32[32,1152,1]{1,2,0:T(1,128)S(1)} async-done(((f32[32,1152,1]{1,2,0:T(1,128)}), f32[32,1152,1]{1,2,0:T(1,128)S(1)}, u32[]{:S(2)}, u32[]{:S(2)}) %all-to-all-start) | async-done | bytes 147488 | tf_op jit(solution)/shard_map/all_to_all | solution.py:406
  28.0 4.6 %pairs.1 = (f32[6,64]{1,0:T(8,128)}, f32[3,128]{1,0:T(4,128)}) custom-call(s32[1]{0:T(128)S(6)} %copy.10.live_ref, f32[288,128]{1,0:T(8,128)S(1)} %bitcast.2, f32[16,128]{1,0:T(8,128)S(1)} %get-tuple-element.25.own_ref, f32[6,192,128]{2,1,0:T(8,128)S(1)} %get-tuple-element.28.column_ref), custom_call_target="tpu_custom_call" | custom-call | tf_op jit(solution)/shard_map/pairs/pallas_call | solution.py:418
Async XLA Ops:
  0.6 6.4 %copy-start = (f32[3,12,24,256]{3,2,1,0:T(8,128)S(1)}, f32[3,12,24,256]{3,2,1,0:T(8,128)}, u32[]{:S(2)}) copy-start(f32[3,12,24,256]{3,2,1,0:T(8,128)} %v_ref.5) | copy-start | bytes 2654212
  1.9 6.7 %collective-permute-start = (f32[3,24,256]{2,1,0:T(8,128)S(1)}, f32[3,24,256]{2,1,0:T(8,128)S(1)}, u32[]{:S(2)}, u32[]{:S(2)}) collective-permute-start(f32[3,24,256]{2,1,0:T(8,128)S(1)} %get-tuple-element.17), channel_id=1, source_target_pairs={{0,4},{8,12},{16,20},{24,28},{4,0},{12,8},{20,16},{28,24},{1,5},{9... | collective-permute-start | bytes 221192 | tf_op jit(solution)/shard_map/ppermute | solution.py:386
  5.0 3.7 %collective-permute-start.1 = (f32[3,24,256]{2,1,0:T(8,128)S(1)}, f32[3,24,256]{2,1,0:T(8,128)S(1)}, u32[]{:S(2)}, u32[]{:S(2)}) collective-permute-start(f32[3,24,256]{2,1,0:T(8,128)S(1)} %get-tuple-element.18), channel_id=1, source_target_pairs={{4,8},{12,16},{20,24},{8,4},{16,12},{24,20},{5,9},{13,17},{21,25},... | collective-permute-start | bytes 221192 | tf_op jit(solution)/shard_map/ppermute | solution.py:387
  5.7 3.0 %collective-permute-start.2 = (f32[3,12,256]{2,1,0:T(8,128)S(1)}, f32[3,12,256]{2,1,0:T(8,128)S(1)}, u32[]{:S(2)}, u32[]{:S(2)}) collective-permute-start(f32[3,12,256]{2,1,0:T(8,128)S(1)} %get-tuple-element.19), channel_id=1, source_target_pairs={{0,1},{2,3},{1,0},{3,2},{4,5},{6,7},{5,4},{7,6},{8,9},{10,11},{9,8... | collective-permute-start | bytes 110600 | tf_op jit(solution)/shard_map/ppermute | solution.py:388
  5.7 2.9 %collective-permute-start.3 = (f32[3,12,256]{2,1,0:T(8,128)S(1)}, f32[3,12,256]{2,1,0:T(8,128)S(1)}, u32[]{:S(2)}, u32[]{:S(2)}) collective-permute-start(f32[3,12,256]{2,1,0:T(8,128)S(1)} %get-tuple-element.20), channel_id=1, source_target_pairs={{1,2},{2,1},{5,6},{6,5},{9,10},{10,9},{13,14},{14,13},{17,18},{18,... | collective-permute-start | bytes 110600 | tf_op jit(solution)/shard_map/ppermute | solution.py:389
  9.6 18.5 %all-to-all-start = ((f32[32,1152,1]{1,2,0:T(1,128)}), f32[32,1152,1]{1,2,0:T(1,128)S(1)}, u32[]{:S(2)}, u32[]{:S(2)}) async-start(f32[32,1152,1]{1,2,0:T(1,128)} %bitcast.3), calls=%async_computation | async-start | bytes 294912 | tf_op jit(solution)/shard_map/all_to_all | solution.py:406
where the time goes:
time: 32.9 us; the launch traced here: 32.7 us
  starting transfers between devices  14.5 us (44%)
  Pallas kernels  10.9 us (33%)
  waiting for transfers between devices  5.88 us (18%)
  between operations  1.37 us (4%)
    all_to_all x1, starting transfers between devices, per_device(): lax.all_to_all(block.reshape(-1), everyone, 0, 0, tiled=True)  10.1 us
    all_to_all x1, waiting for transfers between devices, per_device(): lax.all_to_all(block.reshape(-1), everyone, 0, 0, tiled=True)  5.86 us
    pallas_call x1, Pallas kernels, per_device(): pl.pallas_call(functools.partial(pair_kernel, cells=(cells_x, cells_y, ce...  4.6 us
    ppermute x1, starting transfers between devices, per_device(): xa = held(lax.ppermute(xa, 'tgt', partners(x_count, 0)))  3.06 us
    pallas_call x1, Pallas kernels, per_device(): pl.pallas_call(grid_kernel, name='grid', out_shape=(jax.ShapeDtypeStruct(...  2.55 us
    pallas_call x1, Pallas kernels, per_device(): pl.pallas_call(local_kernel, name='local', out_shape=(kept(8, cells_z), k...  1.59 us
    pallas_call x1, Pallas kernels, per_device(): pl.pallas_call(faces_kernel, name='faces', out_shape=(kept(3, cells_y, ce...  1.29 us
    pallas_call x1, Pallas kernels, per_device(): pl.pallas_call(block_kernel, name='block', out_shape=(jax.ShapeDtypeStruc...  0.87 us
  transfers between devices with their start and end apart: 5, of which 1 were waited for; matrix products, arithmetic and copies ran while one was open for 0% of the time, Pallas kernels for 13%

commit v1 on v0

--- a/solution.py
+++ b/solution.py
@@ -16,7 +16,6 @@
 
 
 VMEM = pl.BlockSpec(memory_space=pltpu.VMEM)
-SMEM = pl.BlockSpec(memory_space=pltpu.SMEM)
 
 
 def split3(value):
@@ -59,6 +58,15 @@
     x_index = lax.axis_index("tgt")
     y_index = lax.axis_index("src") * lax.axis_size("grp") + lax.axis_index("grp")
     return x_index, y_index
+
+
+def middle(cells):
+    x_index, y_index = here()
+    return [
+        (x_index.astype(jnp.float32) + 0.5) * (cells[0] / cells[2]),
+        (y_index.astype(jnp.float32) + 0.5) * (cells[1] / cells[2]),
+        0.5,
+    ]
 
 
 def faces_kernel(v_ref, xa_ref, xb_ref, ya_ref, yb_ref, low_ref, high_ref, sems):
@@ -154,8 +162,9 @@
     row_ref[0:1, :] = (blobs[1:2] * inverse + x_anchor) / cells_z
     row_ref[1:2, :] = (blobs[2:3] * inverse + y_anchor) / cells_z
     row_ref[2:3, :] = (blobs[3:4] * inverse) / cells_z
-    alive = lax.broadcasted_iota(jnp.int32, (3, slot_count), 1) < live_ref[0]
-    strength = jnp.where(alive, strength_ref[...], 0.0)
+    alive = lax.broadcasted_iota(jnp.int32, (1, LANES), 1) < live_ref[...]
+    row_ref[6:7, :] = jnp.where(alive, 1.0, 0.0)
+    strength = jnp.where(alive[:, 0:slot_count], strength_ref[...], 0.0)
     parts = [position_ref[k : k + 1] for k in range(3)] + [strength[k : k + 1] for k in range(3)]
     for k in range(3):
         row_ref[3 + k : 4 + k, :] = jnp.concatenate(parts[2 * k : 2 * k + 2], axis=1)
@@ -179,6 +188,7 @@
     strength = seed_weight * pair_lanes(total)
     block = jnp.concatenate([row_ref[0:3], strength[0:3], row_ref[3:6]], axis=0)
     own_ref[0:GROUPS, :] = block
+    own_ref[GROUPS : GROUPS + 1, :] = row_ref[6:7, :]
     devices = out_ref.shape[0] // GROUPS
     for device in range(devices):
         out_ref[device * GROUPS : (device + 1) * GROUPS, :] = block
@@ -193,7 +203,7 @@
     return rows
 
 
-def grid_kernel(v_ref, d_ref, xa_ref, xb_ref, ya_ref, yb_ref, own_ref, out_ref, column_ref):
+def grid_kernel(v_ref, d_ref, xa_ref, xb_ref, ya_ref, yb_ref, own_ref, out_ref, column_ref, factor_ref):
     _, cells_x, cells_y, cells_z = v_ref.shape
     x_index, y_index = here()
     x_even = lax.rem(x_index, 2) == 0
@@ -214,30 +224,45 @@
             out_ref[k, x] = v + d_ref[x] * (beside - 6.0 * v)
 
     own = own_ref[0:GROUPS, :]
+    centre = middle((cells_x, cells_y, cells_z))
     particles = target_rows(own)
     zeros = jnp.zeros((1, LANES), jnp.float32)
-    wide = [jnp.concatenate([own[k : k + 1], particles[k]], axis=1) for k in range(3)]
-    wide = wide + [jnp.concatenate([zeros, particles[k]], axis=1) for k in range(3, 6)]
-    table = jnp.concatenate(wide + [jnp.zeros((LANES - 6, 2 * LANES), jnp.float32)], axis=0)
-    columns = jnp.transpose(table)
+    place = [own[k : k + 1] - centre[k] for k in range(2)]
+    slot_place = [particles[k] - centre[k] for k in range(3)]
+    a = particles[3:]
+    along = a[0] * slot_place[0] + a[1] * slot_place[1] + a[2] * slot_place[2]
+    factors = [
+        jnp.concatenate([-2.0 * place[0], -a[0]], axis=1),
+        jnp.concatenate([-2.0 * place[1], -a[1]], axis=1),
+        jnp.concatenate([zeros, -a[2]], axis=1),
+        jnp.concatenate([place[0] * place[0] + place[1] * place[1], along], axis=1),
+    ]
+    factors = [[part.astype(jnp.float32) for part in split3(factor)] for factor in factors]
+    nothing = jnp.zeros((1, 2 * LANES), jnp.float32)
+    ones = jnp.concatenate([zeros + 1.0, zeros], axis=1)
+    table = []
+    for j in range(3):
+        for k in range(3):
+            table += [factors[k][j]] * 3
+        table += [ones if j == 0 else nothing] * 3
+        table += [factors[3][j]] + [nothing] * 3
+    table += [jnp.concatenate([own[k : k + 1], particles[k]], axis=1) for k in range(3)]
+    table += [nothing] * (LANES - len(table))
+    columns = jnp.transpose(jnp.concatenate(table, axis=0))
     targets = column_ref.shape[1]
-    for k in range(6):
-        begin = 0 if k < 3 else LANES
-        column_ref[k, begin:targets, :] = jnp.broadcast_to(columns[begin:targets, k : k + 1], (targets - begin, LANES))
-
-
-def pair_kernel(live_ref, all_ref, own_ref, column_ref, rates_ref, blob_ref, source_ref, feature_ref, turn_ref, sum_ref, *, cells):
+    factor_ref[...] = columns[0:targets].astype(jnp.bfloat16)
+    for k in range(3):
+        begin = LANES if k < 2 else 0
+        column_ref[k, begin:targets, :] = jnp.broadcast_to(columns[begin:targets, 48 + k : 49 + k], (targets - begin, LANES))
+
+
+def pair_kernel(all_ref, own_ref, column_ref, factor_ref, rates_ref, blob_ref, source_ref, coordinate_ref, feature_ref, turn_ref, flat_ref, sum_ref, *, cells):
     devices = all_ref.shape[0] // GROUPS
     half = LANES // 2
     tiles = devices + devices // 2
     targets = column_ref.shape[1]
     lane = lax.broadcasted_iota(jnp.int32, (devices, LANES), 1)
-    x_index, y_index = here()
-    centre = [
-        (x_index.astype(jnp.float32) + 0.5) * (cells[0] / cells[2]),
-        (y_index.astype(jnp.float32) + 0.5) * (cells[1] / cells[2]),
-        0.5,
-    ]
+    centre = middle(cells)
 
     def group(index):
         return all_ref[pl.ds(index, devices, stride=GROUPS), :]
@@ -270,58 +295,75 @@
             row = (8 * j + k) * tiles
             feature_ref[row : row + tiles, :] = parts[j].astype(jnp.float32)
 
+    flat = place[0] * place[0] + place[1] * place[1] + sigma_sq
+    for k, value in enumerate(place + [flat]):
+        parts = split3(value)
+        for j in range(3):
+            row = (3 * k + j) * tiles
+            coordinate_ref[row : row + tiles, :] = parts[j].astype(jnp.float32)
+    coordinate_ref[12 * tiles : 13 * tiles, :] = jnp.ones((tiles, LANES), jnp.float32)
+    coordinate_ref[13 * tiles :, :] = jnp.zeros((3 * tiles, LANES), jnp.float32)
+
     sum_ref[...] = jnp.zeros_like(sum_ref)
-    block = 32
+    factors = factor_ref[:, 0:48]
+    block = half
     width = 4 if tiles % 4 == 0 else 1
     steps = tiles // width
-    unroll = next(n for n in (12, 8, 6, 4, 3, 2, 1) if steps % n == 0)
+    unroll = next(n for n in (12, 8, 6, 4, 2, steps) if steps % n == 0 and (n % 2 == 0 or n == steps))
     contract = (((1,), (1,)), ((), ()))
 
     def product(values, feature):
         highs = [value.astype(jnp.bfloat16) for value in values]
         lows = [(value - high.astype(jnp.float32)).astype(jnp.bfloat16) for value, high in zip(values, highs)]
         both = jnp.concatenate([jnp.concatenate(highs, axis=1), jnp.concatenate(lows, axis=1)], axis=0)
-        return lax.dot_general(both, feature, contract, preferred_element_type=jnp.float32)
-
-    def one(chunk):
+        return lax.dot_general(feature, both, contract, preferred_element_type=jnp.float32)
+
+    def ahead(chunk, slot):
+        spans = [chunk * width + j for j in range(width)]
+        coordinate = jnp.concatenate([coordinate_ref[pl.ds(tile, 16, stride=tiles), :].astype(jnp.bfloat16) for tile in spans], axis=1)
+        flat_ref[slot] = jnp.dot(factors, jnp.concatenate([coordinate] * 3, axis=0), preferred_element_type=jnp.float32)
+
+    def one(chunk, slot):
         spans = [chunk * width + j for j in range(width)]
         feature = jnp.concatenate([feature_ref[pl.ds(tile, 32, stride=tiles), :].astype(jnp.bfloat16) for tile in spans], axis=1)
+        ahead(jnp.minimum(chunk + 1, steps - 1), 1 - slot)
         source = [[source_ref[pl.ds(k * tiles + tile, 1), :] for k in range(3)] for tile in spans]
         for t in range(0, targets, block):
             kernels, pulls = [], []
             for j in range(width):
-                sep = [column_ref[k, t : t + block, :] - source[j][k] for k in range(3)]
-                squared = sep[0] * sep[0] + sep[1] * sep[1] + (sep[2] * sep[2] + sigma_sq)
+                known = flat_ref[slot, t : t + block, j * LANES : (j + 1) * LANES]
+                deep = column_ref[2, t : t + block, :] - source[j][2]
+                if t < LANES:
+                    squared = deep * deep + known
+                else:
+                    sep = [column_ref[k, t : t + block, :] - source[j][k] for k in range(2)]
+                    squared = sep[0] * sep[0] + sep[1] * sep[1] + (deep * deep + sigma_sq)
                 inverse = lax.rsqrt(squared)
                 square = inverse * inverse
                 kernel = square * inverse
                 kernels.append(kernel)
                 if t >= LANES:
-                    along = column_ref[3, t : t + block, :] * sep[0] + column_ref[4, t : t + block, :] * sep[1] + column_ref[5, t : t + block, :] * sep[2]
-                    pulls.append((kernel * square) * along)
-            rows = slice(2 * t, 2 * t + 2 * block)
-            sum_ref[rows, 0:32] = sum_ref[rows, 0:32] + product(kernels, feature)
+                    pulls.append((kernel * square) * known)
+            sum_ref[t // block] = sum_ref[t // block] + product(kernels, feature)
             if t >= LANES:
-                rows = slice(2 * (targets + t - LANES), 2 * (targets + t - LANES) + 2 * block)
-                sum_ref[rows, 0:32] = sum_ref[rows, 0:32] + product(pulls, feature)
+                sum_ref[3] = sum_ref[3] + product(pulls, feature)
 
     def step(index, _):
         for j in range(unroll):
-            one(index * unroll + j)
+            one(index * unroll + j, j % 2)
         return 0
 
+    ahead(0, 0)
     lax.fori_loop(0, steps // unroll, step, 0)
 
-    def combined(begin, end):
-        parts = [sum_ref[2 * t : 2 * t + block] + sum_ref[2 * t + block : 2 * t + 2 * block] for t in range(begin, end, block)]
-        rest = -(end - begin) % LANES
-        if rest:
-            parts.append(jnp.zeros((rest, LANES), jnp.float32))
-        turned = jnp.transpose(jnp.concatenate(parts, axis=0))
-        return turned[0:8] + turned[8:16] + turned[16:24]
-
-    found = combined(0, targets)
-    pulled = combined(targets, targets + half)
+    def combined(index):
+        parts = sum_ref[index, 0:8] + sum_ref[index, 8:16] + sum_ref[index, 16:24]
+        return parts + pltpu.roll(parts, block, 1)
+
+    lane = lax.broadcasted_iota(jnp.int32, (8, LANES), 1)
+    found = jnp.where(lane < block, combined(0), combined(1))
+    near = combined(2)
+    pulled = combined(3)
 
     def crossed(place, rows):
         return [
@@ -332,8 +374,7 @@
 
     own = own_ref[0:GROUPS, :]
     slots = target_rows(own)
-    near = found[:, LANES:]
-    alive = (lax.broadcasted_iota(jnp.int32, (1, LANES), 1) < live_ref[0]).astype(jnp.float32)
+    alive = own_ref[GROUPS : GROUPS + 1, :]
     blob_place = [own[k : k + 1] - centre[k] for k in range(3)]
     slot_place = [slots[k] - centre[k] for k in range(3)]
     a = slots[3:]
@@ -342,7 +383,7 @@
         a[2] * near[0:1] - a[0] * near[2:3],
         a[0] * near[1:2] - a[1] * near[0:1],
     ]
-    blob_velocity = crossed(blob_place, found[:, 0:LANES])
+    blob_velocity = crossed(blob_place, found)
     slot_velocity = crossed(slot_place, near)
     second = crossed(slot_place, pulled)
     for k in range(3):
@@ -393,9 +434,9 @@
         local_kernel,
         name="local",
         out_shape=(kept(8, cells_z), kept(2, cells_y, cells_z), kept(2, cells_x, cells_z), kept(8, LANES)),
-        in_specs=[SMEM] + [VMEM] * 5,
+        in_specs=[VMEM] * 6,
         out_specs=[VMEM] * 4,
-    )(live_counts, v, d, c, positions, strengths)
+    )(live_counts.reshape(1, 1), v, d, c, positions, strengths)
     block, own = pl.pallas_call(
         block_kernel,
         name="block",
@@ -406,12 +447,12 @@
     everything = lax.all_to_all(block.reshape(-1), everyone, 0, 0, tiled=True).reshape(devices * GROUPS, LANES)
 
     targets = LANES + slot_count
-    vorticity_next, columns = pl.pallas_call(
+    vorticity_next, columns, factors = pl.pallas_call(
         grid_kernel,
         name="grid",
-        out_shape=(jax.ShapeDtypeStruct(vorticity.shape, f32), kept(6, targets, LANES)),
+        out_shape=(jax.ShapeDtypeStruct(vorticity.shape, f32), kept(3, targets, LANES), pltpu.VMEM((targets, LANES), jnp.bfloat16)),
         in_specs=[VMEM] * 7,
-        out_specs=[VMEM] * 2,
+        out_specs=[VMEM] * 3,
     )(v, d, xa, xb, ya, yb, held(own))
 
     tiles = devices + devices // 2
@@ -419,15 +460,17 @@
         functools.partial(pair_kernel, cells=(cells_x, cells_y, cells_z)),
         name="pairs",
         out_shape=(jax.ShapeDtypeStruct((6, slot_count), f32), jax.ShapeDtypeStruct((3, LANES), f32)),
-        in_specs=[SMEM] + [VMEM] * 3,
+        in_specs=[VMEM] * 4,
         out_specs=[VMEM, VMEM],
         scratch_shapes=[
             pltpu.VMEM((3 * tiles, LANES), f32),
+            pltpu.VMEM((16 * tiles, LANES), f32),
             pltpu.VMEM((32 * tiles, LANES), f32),
             pltpu.VMEM((devices, LANES), f32),
-            pltpu.VMEM((2 * targets + 2 * slot_count, LANES), f32),
+            pltpu.VMEM((2, targets, 4 * LANES), f32),
+            pltpu.VMEM((4, 32, LANES), f32),
         ],
-    )(live_counts, held(everything), held(own), held(columns))
+    )(held(everything), held(own), held(columns), held(factors))
     return (vorticity_next, particle_rates, blob_velocity)
 
 

time: 32.9 us -> 32 us (0.973)
  Pallas kernels: 10.9 us -> 9.91 us
    pallas_call x1, Pallas kernels: 4.6 us -> 3.67 us  [per_device(): pl.pallas_call(functools.partial(pair_kernel, cells=(cells_x, cells_y, ce...]
where the time goes in v1:
time: 32 us; the launch traced here: 31.7 us
  starting transfers between devices  14.5 us (45%)
  Pallas kernels  9.91 us (31%)
  waiting for transfers between devices  5.93 us (19%)
  between operations  1.37 us (4%)
    all_to_all x1, starting transfers between devices, per_device(): lax.all_to_all(block.reshape(-1), everyone, 0, 0, tiled=True)  10 us
    all_to_all x1, waiting for transfers between devices, per_device(): lax.all_to_all(block.reshape(-1), everyone, 0, 0, tiled=True)  5.92 us
    pallas_call x1, Pallas kernels, per_device(): pl.pallas_call(functools.partial(pair_kernel, cells=(cells_x, cells_y, ce...  3.67 us
    ppermute x1, starting transfers between devices, per_device(): xa = held(lax.ppermute(xa, 'tgt', partners(x_count, 0)))  3.06 us
    pallas_call x1, Pallas kernels, per_device(): pl.pallas_call(grid_kernel, name='grid', out_shape=(jax.ShapeDtypeStruct(...  2.49 us
    pallas_call x1, Pallas kernels, per_device(): pl.pallas_call(local_kernel, name='local', out_shape=(kept(8, cells_z), k...  1.59 us
    pallas_call x1, Pallas kernels, per_device(): pl.pallas_call(faces_kernel, name='faces', out_shape=(kept(3, cells_y, ce...  1.29 us
    pallas_call x1, Pallas kernels, per_device(): pl.pallas_call(block_kernel, name='block', out_shape=(jax.ShapeDtypeStruc...  0.87 us
  transfers between devices with their start and end apart: 5, of which 1 were waited for; matrix products, arithmetic and copies ran while one was open for 0% of the time, Pallas kernels for 13%

profile of v1, /device:TPU:0, one launch (start us, length us, event | category | flops | bytes accessed | tf_op | source)
XLA Modules:
  0.0 31.7 jit_solution(15164134576345732565)
XLA Ops:
  0.6 0.0 copy-start
  0.6 1.3 %faces.1 = (f32[3,24,256]{2,1,0:T(8,128)S(1)}, f32[3,24,256]{2,1,0:T(8,128)S(1)}, f32[3,12,256]{2,1,0:T(8,128)S(1)}, f32[3,12,256]{2,1,0:T(8,128)S(1)}) custom-call(f32[3,12,24,256]{3,2,1,0:T(8,128)} %v_ref.5), custom_call_target="tpu_custom_call" | custom-call | tf_op jit(solution)/shard_map/faces/pallas_call | solution.py:415
  1.9 3.1 %collective-permute-start = (f32[3,24,256]{2,1,0:T(8,128)S(1)}, f32[3,24,256]{2,1,0:T(8,128)S(1)}, u32[]{:S(2)}, u32[]{:S(2)}) collective-permute-start(f32[3,24,256]{2,1,0:T(8,128)S(1)} %get-tuple-element.18), channel_id=1, source_target_pairs={{0,4},{8,12},{16,20},{24,28},{4,0},{12,8},{20,16},{28,24},{1,5},{9... | collective-permute-start | bytes 221192 | tf_op jit(solution)/shard_map/ppermute | solution.py:427
  5.0 0.7 %collective-permute-start.1 = (f32[3,24,256]{2,1,0:T(8,128)S(1)}, f32[3,24,256]{2,1,0:T(8,128)S(1)}, u32[]{:S(2)}, u32[]{:S(2)}) collective-permute-start(f32[3,24,256]{2,1,0:T(8,128)S(1)} %get-tuple-element.19), channel_id=1, source_target_pairs={{4,8},{12,16},{20,24},{8,4},{16,12},{24,20},{5,9},{13,17},{21,25},... | collective-permute-start | bytes 221192 | tf_op jit(solution)/shard_map/ppermute | solution.py:428
  5.7 0.1 collective-permute-start.2
  5.7 0.7 %collective-permute-start.3 = (f32[3,12,256]{2,1,0:T(8,128)S(1)}, f32[3,12,256]{2,1,0:T(8,128)S(1)}, u32[]{:S(2)}, u32[]{:S(2)}) collective-permute-start(f32[3,12,256]{2,1,0:T(8,128)S(1)} %get-tuple-element.21), channel_id=1, source_target_pairs={{1,2},{2,1},{5,6},{6,5},{9,10},{10,9},{13,14},{14,13},{17,18},{18,... | collective-permute-start | bytes 110600 | tf_op jit(solution)/shard_map/ppermute | solution.py:430
  7.1 0.0 copy-done
  7.1 1.6 %local.1 = (f32[8,256]{1,0:T(8,128)S(1)}, f32[2,24,256]{2,1,0:T(8,128)S(1)}, f32[2,12,256]{2,1,0:T(8,128)S(1)}, f32[8,128]{1,0:T(8,128)S(1)}) custom-call(s32[1,1]{1,0:T(1,128)} %bitcast.3.live_ref, f32[3,12,24,256]{3,2,1,0:T(8,128)S(1)} %copy-done, f32[12,24,256]{2,1,0:T(8,128)} %d_ref.3, s32[12,24,256]{2,1,0:T(8,128)} %c_ref.1, f32[3,64]{1,0:T(4,128)} %position_ref.1, ...), custom_call_target="tpu_custom_call" | custom-call | tf_op jit(solution)/shard_map/local/pallas_call | solution.py:433
  8.7 0.0 collective-permute-done.2.ya_ref
  8.7 0.0 collective-permute-done.3.yb_ref
  8.7 0.0 collective-permute-done.xa_ref
  8.7 0.0 collective-permute-done.1.xb_ref
  8.7 0.9 %block.1 = (f32[288,128]{1,0:T(8,128)}, f32[16,128]{1,0:T(8,128)S(1)}) custom-call(f32[8,256]{1,0:T(8,128)S(1)} %get-tuple-element.22.sums_ref, f32[2,24,256]{2,1,0:T(8,128)S(1)} %get-tuple-element.23.wx_ref, f32[2,12,256]{2,1,0:T(8,128)S(1)} %get-tuple-element.24.wy_ref, f32[8,128]{1,0:T(8,128)S(1)} %get-tuple-element.25.row_ref, ...), custom_call_target="tpu_custom_call" | custom-call | tf_op jit(solution)/shard_map/block/pallas_call | solution.py:440
  9.6 10.0 %all-to-all-start = ((f32[32,1152,1]{1,2,0:T(1,128)}), f32[32,1152,1]{1,2,0:T(1,128)S(1)}, u32[]{:S(2)}, u32[]{:S(2)}) async-start(f32[32,1152,1]{1,2,0:T(1,128)} %bitcast.5), calls=%async_computation | async-start | bytes 294912 | tf_op jit(solution)/shard_map/all_to_all | solution.py:447
  19.6 2.5 %grid.1 = (f32[3,12,24,256]{3,2,1,0:T(8,128)}, f32[3,192,128]{2,1,0:T(8,128)S(1)}, bf16[192,128]{1,0:T(8,128)(2,1)S(1)}) custom-call(f32[3,12,24,256]{3,2,1,0:T(8,128)S(1)} %copy-done, f32[12,24,256]{2,1,0:T(8,128)} %d_ref.3, f32[3,24,256]{2,1,0:T(8,128)S(1)} %collective-permute-done.xa_ref, f32[3,24,256]{2,1,0:T(8,128)S(1)} %collective-permute-done.1.xb_ref, ...), custom_call_target="tpu_custom_call" | custom-call | tf_op jit(solution)/shard_map/grid/pallas_call | solution.py:450
  22.1 5.9 %all-to-all-done = f32[32,1152,1]{1,2,0:T(1,128)S(1)} async-done(((f32[32,1152,1]{1,2,0:T(1,128)}), f32[32,1152,1]{1,2,0:T(1,128)S(1)}, u32[]{:S(2)}, u32[]{:S(2)}) %all-to-all-start) | async-done | bytes 147488 | tf_op jit(solution)/shard_map/all_to_all | solution.py:447
  28.0 3.7 %pairs.1 = (f32[6,64]{1,0:T(8,128)}, f32[3,128]{1,0:T(4,128)}) custom-call(f32[288,128]{1,0:T(8,128)S(1)} %bitcast.4, f32[16,128]{1,0:T(8,128)S(1)} %get-tuple-element.26.own_ref, f32[3,192,128]{2,1,0:T(8,128)S(1)} %get-tuple-element.29.column_ref, bf16[192,128]{1,0:T(8,128)(2,1)S(1)} %get-tuple-element.30.factor_ref), custom_call_target="tpu_custom_call" | custom-call | tf_op jit(solution)/shard_map/pairs/pallas_call | solution.py:459
Async XLA Ops:
  0.6 6.4 %copy-start = (f32[3,12,24,256]{3,2,1,0:T(8,128)S(1)}, f32[3,12,24,256]{3,2,1,0:T(8,128)}, u32[]{:S(2)}) copy-start(f32[3,12,24,256]{3,2,1,0:T(8,128)} %v_ref.5) | copy-start | bytes 2654212
  1.9 6.7 %collective-permute-start = (f32[3,24,256]{2,1,0:T(8,128)S(1)}, f32[3,24,256]{2,1,0:T(8,128)S(1)}, u32[]{:S(2)}, u32[]{:S(2)}) collective-permute-start(f32[3,24,256]{2,1,0:T(8,128)S(1)} %get-tuple-element.18), channel_id=1, source_target_pairs={{0,4},{8,12},{16,20},{24,28},{4,0},{12,8},{20,16},{28,24},{1,5},{9... | collective-permute-start | bytes 221192 | tf_op jit(solution)/shard_map/ppermute | solution.py:427
  5.0 3.7 %collective-permute-start.1 = (f32[3,24,256]{2,1,0:T(8,128)S(1)}, f32[3,24,256]{2,1,0:T(8,128)S(1)}, u32[]{:S(2)}, u32[]{:S(2)}) collective-permute-start(f32[3,24,256]{2,1,0:T(8,128)S(1)} %get-tuple-element.19), channel_id=1, source_target_pairs={{4,8},{12,16},{20,24},{8,4},{16,12},{24,20},{5,9},{13,17},{21,25},... | collective-permute-start | bytes 221192 | tf_op jit(solution)/shard_map/ppermute | solution.py:428
  5.7 3.0 %collective-permute-start.2 = (f32[3,12,256]{2,1,0:T(8,128)S(1)}, f32[3,12,256]{2,1,0:T(8,128)S(1)}, u32[]{:S(2)}, u32[]{:S(2)}) collective-permute-start(f32[3,12,256]{2,1,0:T(8,128)S(1)} %get-tuple-element.20), channel_id=1, source_target_pairs={{0,1},{2,3},{1,0},{3,2},{4,5},{6,7},{5,4},{7,6},{8,9},{10,11},{9,8... | collective-permute-start | bytes 110600 | tf_op jit(solution)/shard_map/ppermute | solution.py:429
  5.7 2.9 %collective-permute-start.3 = (f32[3,12,256]{2,1,0:T(8,128)S(1)}, f32[3,12,256]{2,1,0:T(8,128)S(1)}, u32[]{:S(2)}, u32[]{:S(2)}) collective-permute-start(f32[3,12,256]{2,1,0:T(8,128)S(1)} %get-tuple-element.21), channel_id=1, source_target_pairs={{1,2},{2,1},{5,6},{6,5},{9,10},{10,9},{13,14},{14,13},{17,18},{18,... | collective-permute-start | bytes 110600 | tf_op jit(solution)/shard_map/ppermute | solution.py:430
  9.6 18.5 %all-to-all-start = ((f32[32,1152,1]{1,2,0:T(1,128)}), f32[32,1152,1]{1,2,0:T(1,128)S(1)}, u32[]{:S(2)}, u32[]{:S(2)}) async-start(f32[32,1152,1]{1,2,0:T(1,128)} %bitcast.5), calls=%async_computation | async-start | bytes 294912 | tf_op jit(solution)/shard_map/all_to_all | solution.py:447

commit v2 on v1

--- a/solution.py
+++ b/solution.py
@@ -74,21 +74,20 @@
     x_index, y_index = here()
     x_even = lax.rem(x_index, 2) == 0
     y_even = lax.rem(y_index, 2) == 0
-    top = (cells_y - 1) // 8 * 8
     last = cells_x - 1
     copies = [
         pltpu.make_async_copy(v_ref.at[:, jnp.where(x_even, 0, last)], xb_ref, sems.at[0]),
         pltpu.make_async_copy(v_ref.at[:, jnp.where(x_even, last, 0)], xa_ref, sems.at[1]),
-        pltpu.make_async_copy(v_ref.at[:, :, 0:8], low_ref, sems.at[2]),
-        pltpu.make_async_copy(v_ref.at[:, :, top : top + 8], high_ref, sems.at[3]),
+        pltpu.make_async_copy(v_ref.at[:, :, 0:1], low_ref, sems.at[2]),
+        pltpu.make_async_copy(v_ref.at[:, :, cells_y - 1 : cells_y], high_ref, sems.at[3]),
     ]
-    for copy in copies:
+    for copy in copies[2:] + copies[:2]:
         copy.start()
     copies[2].wait()
     copies[3].wait()
     for k in range(3):
         first = low_ref[k, :, 0, :]
-        final = high_ref[k, :, cells_y - 1 - top, :]
+        final = high_ref[k, :, 0, :]
         ya_ref[k] = jnp.where(y_even, final, first)
         yb_ref[k] = jnp.where(y_even, first, final)
     copies[0].wait()
@@ -419,8 +418,8 @@
         in_specs=[pl.BlockSpec(memory_space=pl.ANY)],
         out_specs=[VMEM] * 4,
         scratch_shapes=[
-            pltpu.VMEM((3, cells_x, 8, cells_z), f32),
-            pltpu.VMEM((3, cells_x, 8, cells_z), f32),
+            pltpu.VMEM((3, cells_x, 1, cells_z), f32),
+            pltpu.VMEM((3, cells_x, 1, cells_z), f32),
             pltpu.SemaphoreType.DMA((4,)),
         ],
     )(vorticity)
@@ -429,7 +428,7 @@
     ya = held(lax.ppermute(ya, y_axes, partners(y_count, 0)))
     yb = held(lax.ppermute(yb, y_axes, partners(y_count, 1)))
 
-    v, d, c = held(vorticity), diffusivity, seed_counts
+    v, d, c = vorticity, diffusivity, seed_counts
     sums, wx, wy, rows = pl.pallas_call(
         local_kernel,
         name="local",

time: 32 us -> 31.7 us (level)
  transfers between devices with their start and end apart: 5 -> 5, of which waited for: 1 -> 1; matrix products, arithmetic and copies ran while one was open for 0% -> 0% of each run, Pallas kernels for 13% -> 15%
where the time goes in v2:
time: 31.7 us; the launch traced here: 31.4 us
  starting transfers between devices  14.2 us (45%)
  Pallas kernels  10.2 us (32%)
  waiting for transfers between devices  5.68 us (18%)
  between operations  1.36 us (4%)
    all_to_all x1, starting transfers between devices, per_device(): lax.all_to_all(block.reshape(-1), everyone, 0, 0, tiled=True)  9.78 us
    all_to_all x1, waiting for transfers between devices, per_device(): lax.all_to_all(block.reshape(-1), everyone, 0, 0, tiled=True)  5.67 us
    pallas_call x1, Pallas kernels, per_device(): pl.pallas_call(functools.partial(pair_kernel, cells=(cells_x, cells_y, ce...  3.68 us
    ppermute x1, starting transfers between devices, per_device(): xa = held(lax.ppermute(xa, 'tgt', partners(x_count, 0)))  3.06 us
    pallas_call x1, Pallas kernels, per_device(): pl.pallas_call(grid_kernel, name='grid', out_shape=(jax.ShapeDtypeStruct(...  2.74 us
    pallas_call x1, Pallas kernels, per_device(): pl.pallas_call(local_kernel, name='local', out_shape=(kept(8, cells_z), k...  1.87 us
    pallas_call x1, Pallas kernels, per_device(): pl.pallas_call(faces_kernel, name='faces', out_shape=(kept(3, cells_y, ce...  1.01 us
    pallas_call x1, Pallas kernels, per_device(): pl.pallas_call(block_kernel, name='block', out_shape=(jax.ShapeDtypeStruc...  0.87 us
  transfers between devices with their start and end apart: 5, of which 1 were waited for; matrix products, arithmetic and copies ran while one was open for 0% of the time, Pallas kernels for 15%

profile of v2, /device:TPU:0, one launch (start us, length us, event | category | flops | bytes accessed | tf_op | source)
XLA Modules:
  0.0 31.4 jit_solution(14092260756518452695)
XLA Ops:
  0.6 1.0 %faces.1 = (f32[3,24,256]{2,1,0:T(8,128)S(1)}, f32[3,24,256]{2,1,0:T(8,128)S(1)}, f32[3,12,256]{2,1,0:T(8,128)S(1)}, f32[3,12,256]{2,1,0:T(8,128)S(1)}) custom-call(f32[3,12,24,256]{3,2,1,0:T(8,128)} %v_ref.5), custom_call_target="tpu_custom_call" | custom-call | tf_op jit(solution)/shard_map/faces/pallas_call | solution.py:414
  1.7 3.1 %collective-permute-start = (f32[3,24,256]{2,1,0:T(8,128)S(1)}, f32[3,24,256]{2,1,0:T(8,128)S(1)}, u32[]{:S(2)}, u32[]{:S(2)}) collective-permute-start(f32[3,24,256]{2,1,0:T(8,128)S(1)} %get-tuple-element.18), channel_id=1, source_target_pairs={{0,4},{8,12},{16,20},{24,28},{4,0},{12,8},{20,16},{28,24},{1,5},{9... | collective-permute-start | bytes 221192 | tf_op jit(solution)/shard_map/ppermute | solution.py:426
  4.7 0.7 %collective-permute-start.1 = (f32[3,24,256]{2,1,0:T(8,128)S(1)}, f32[3,24,256]{2,1,0:T(8,128)S(1)}, u32[]{:S(2)}, u32[]{:S(2)}) collective-permute-start(f32[3,24,256]{2,1,0:T(8,128)S(1)} %get-tuple-element.19), channel_id=1, source_target_pairs={{4,8},{12,16},{20,24},{8,4},{16,12},{24,20},{5,9},{13,17},{21,25},... | collective-permute-start | bytes 221192 | tf_op jit(solution)/shard_map/ppermute | solution.py:427
  5.4 0.1 collective-permute-start.2
  5.5 0.7 %collective-permute-start.3 = (f32[3,12,256]{2,1,0:T(8,128)S(1)}, f32[3,12,256]{2,1,0:T(8,128)S(1)}, u32[]{:S(2)}, u32[]{:S(2)}) collective-permute-start(f32[3,12,256]{2,1,0:T(8,128)S(1)} %get-tuple-element.21), channel_id=1, source_target_pairs={{1,2},{2,1},{5,6},{6,5},{9,10},{10,9},{13,14},{14,13},{17,18},{18,... | collective-permute-start | bytes 110600 | tf_op jit(solution)/shard_map/ppermute | solution.py:429
  6.8 1.9 %local.1 = (f32[8,256]{1,0:T(8,128)S(1)}, f32[2,24,256]{2,1,0:T(8,128)S(1)}, f32[2,12,256]{2,1,0:T(8,128)S(1)}, f32[8,128]{1,0:T(8,128)S(1)}) custom-call(s32[1,1]{1,0:T(1,128)} %bitcast.3.live_ref, f32[3,12,24,256]{3,2,1,0:T(8,128)} %v_ref.5, f32[12,24,256]{2,1,0:T(8,128)} %d_ref.3, s32[12,24,256]{2,1,0:T(8,128)} %c_ref.1, f32[3,64]{1,0:T(4,128)} %position_ref.1, ...), custom_call_target="tpu_custom_call" | custom-call | tf_op jit(solution)/shard_map/local/pallas_call | solution.py:432
  8.6 0.0 collective-permute-done.2.ya_ref
  8.7 0.0 collective-permute-done.3.yb_ref
  8.7 0.0 collective-permute-done.xa_ref
  8.7 0.0 collective-permute-done.1.xb_ref
  8.7 0.9 %block.1 = (f32[288,128]{1,0:T(8,128)}, f32[16,128]{1,0:T(8,128)S(1)}) custom-call(f32[8,256]{1,0:T(8,128)S(1)} %get-tuple-element.22.sums_ref, f32[2,24,256]{2,1,0:T(8,128)S(1)} %get-tuple-element.23.wx_ref, f32[2,12,256]{2,1,0:T(8,128)S(1)} %get-tuple-element.24.wy_ref, f32[8,128]{1,0:T(8,128)S(1)} %get-tuple-element.25.row_ref, ...), custom_call_target="tpu_custom_call" | custom-call | tf_op jit(solution)/shard_map/block/pallas_call | solution.py:439
  9.6 9.8 %all-to-all-start = ((f32[32,1152,1]{1,2,0:T(1,128)}), f32[32,1152,1]{1,2,0:T(1,128)S(1)}, u32[]{:S(2)}, u32[]{:S(2)}) async-start(f32[32,1152,1]{1,2,0:T(1,128)} %bitcast.5), calls=%async_computation | async-start | bytes 294912 | tf_op jit(solution)/shard_map/all_to_all | solution.py:446
  19.4 2.7 %grid.1 = (f32[3,12,24,256]{3,2,1,0:T(8,128)}, f32[3,192,128]{2,1,0:T(8,128)S(1)}, bf16[192,128]{1,0:T(8,128)(2,1)S(1)}) custom-call(f32[3,12,24,256]{3,2,1,0:T(8,128)} %v_ref.5, f32[12,24,256]{2,1,0:T(8,128)} %d_ref.3, f32[3,24,256]{2,1,0:T(8,128)S(1)} %collective-permute-done.xa_ref, f32[3,24,256]{2,1,0:T(8,128)S(1)} %collective-permute-done.1.xb_ref, ...), custom_call_target="tpu_custom_call" | custom-call | tf_op jit(solution)/shard_map/grid/pallas_call | solution.py:449
  22.1 5.7 %all-to-all-done = f32[32,1152,1]{1,2,0:T(1,128)S(1)} async-done(((f32[32,1152,1]{1,2,0:T(1,128)}), f32[32,1152,1]{1,2,0:T(1,128)S(1)}, u32[]{:S(2)}, u32[]{:S(2)}) %all-to-all-start) | async-done | bytes 147488 | tf_op jit(solution)/shard_map/all_to_all | solution.py:446
  27.8 3.7 %pairs.1 = (f32[6,64]{1,0:T(8,128)}, f32[3,128]{1,0:T(4,128)}) custom-call(f32[288,128]{1,0:T(8,128)S(1)} %bitcast.4, f32[16,128]{1,0:T(8,128)S(1)} %get-tuple-element.26.own_ref, f32[3,192,128]{2,1,0:T(8,128)S(1)} %get-tuple-element.29.column_ref, bf16[192,128]{1,0:T(8,128)(2,1)S(1)} %get-tuple-element.30.factor_ref), custom_call_target="tpu_custom_call" | custom-call | tf_op jit(solution)/shard_map/pairs/pallas_call | solution.py:458
Async XLA Ops:
  1.7 7.0 %collective-permute-start = (f32[3,24,256]{2,1,0:T(8,128)S(1)}, f32[3,24,256]{2,1,0:T(8,128)S(1)}, u32[]{:S(2)}, u32[]{:S(2)}) collective-permute-start(f32[3,24,256]{2,1,0:T(8,128)S(1)} %get-tuple-element.18), channel_id=1, source_target_pairs={{0,4},{8,12},{16,20},{24,28},{4,0},{12,8},{20,16},{28,24},{1,5},{9... | collective-permute-start | bytes 221192 | tf_op jit(solution)/shard_map/ppermute | solution.py:426
  4.7 4.0 %collective-permute-start.1 = (f32[3,24,256]{2,1,0:T(8,128)S(1)}, f32[3,24,256]{2,1,0:T(8,128)S(1)}, u32[]{:S(2)}, u32[]{:S(2)}) collective-permute-start(f32[3,24,256]{2,1,0:T(8,128)S(1)} %get-tuple-element.19), channel_id=1, source_target_pairs={{4,8},{12,16},{20,24},{8,4},{16,12},{24,20},{5,9},{13,17},{21,25},... | collective-permute-start | bytes 221192 | tf_op jit(solution)/shard_map/ppermute | solution.py:427
  5.4 3.3 %collective-permute-start.2 = (f32[3,12,256]{2,1,0:T(8,128)S(1)}, f32[3,12,256]{2,1,0:T(8,128)S(1)}, u32[]{:S(2)}, u32[]{:S(2)}) collective-permute-start(f32[3,12,256]{2,1,0:T(8,128)S(1)} %get-tuple-element.20), channel_id=1, source_target_pairs={{0,1},{2,3},{1,0},{3,2},{4,5},{6,7},{5,4},{7,6},{8,9},{10,11},{9,8... | collective-permute-start | bytes 110600 | tf_op jit(solution)/shard_map/ppermute | solution.py:428
  5.5 3.2 %collective-permute-start.3 = (f32[3,12,256]{2,1,0:T(8,128)S(1)}, f32[3,12,256]{2,1,0:T(8,128)S(1)}, u32[]{:S(2)}, u32[]{:S(2)}) collective-permute-start(f32[3,12,256]{2,1,0:T(8,128)S(1)} %get-tuple-element.21), channel_id=1, source_target_pairs={{1,2},{2,1},{5,6},{6,5},{9,10},{10,9},{13,14},{14,13},{17,18},{18,... | collective-permute-start | bytes 110600 | tf_op jit(solution)/shard_map/ppermute | solution.py:429
  9.6 18.2 %all-to-all-start = ((f32[32,1152,1]{1,2,0:T(1,128)}), f32[32,1152,1]{1,2,0:T(1,128)S(1)}, u32[]{:S(2)}, u32[]{:S(2)}) async-start(f32[32,1152,1]{1,2,0:T(1,128)} %bitcast.5), calls=%async_computation | async-start | bytes 294912 | tf_op jit(solution)/shard_map/all_to_all | solution.py:446

commit v3 on v2

--- a/solution.py
+++ b/solution.py
@@ -259,7 +259,7 @@
     devices = all_ref.shape[0] // GROUPS
     half = LANES // 2
     tiles = devices + devices // 2
-    targets = column_ref.shape[1]
+    pitch = tiles + 1 - tiles % 2
     lane = lax.broadcasted_iota(jnp.int32, (devices, LANES), 1)
     centre = middle(cells)
 
@@ -291,17 +291,17 @@
     for k in range(6):
         parts = split3(features[k])
         for j in range(3):
-            row = (8 * j + k) * tiles
+            row = (8 * j + k) * pitch
             feature_ref[row : row + tiles, :] = parts[j].astype(jnp.float32)
 
     flat = place[0] * place[0] + place[1] * place[1] + sigma_sq
     for k, value in enumerate(place + [flat]):
         parts = split3(value)
         for j in range(3):
-            row = (3 * k + j) * tiles
+            row = (3 * k + j) * pitch
             coordinate_ref[row : row + tiles, :] = parts[j].astype(jnp.float32)
-    coordinate_ref[12 * tiles : 13 * tiles, :] = jnp.ones((tiles, LANES), jnp.float32)
-    coordinate_ref[13 * tiles :, :] = jnp.zeros((3 * tiles, LANES), jnp.float32)
+    coordinate_ref[12 * pitch : 12 * pitch + tiles, :] = jnp.ones((tiles, LANES), jnp.float32)
+    coordinate_ref[13 * pitch :, :] = jnp.zeros((3 * pitch, LANES), jnp.float32)
 
     sum_ref[...] = jnp.zeros_like(sum_ref)
     factors = factor_ref[:, 0:48]
@@ -311,41 +311,43 @@
     unroll = next(n for n in (12, 8, 6, 4, 2, steps) if steps % n == 0 and (n % 2 == 0 or n == steps))
     contract = (((1,), (1,)), ((), ()))
 
-    def product(values, feature):
-        highs = [value.astype(jnp.bfloat16) for value in values]
-        lows = [(value - high.astype(jnp.float32)).astype(jnp.bfloat16) for value, high in zip(values, highs)]
-        both = jnp.concatenate([jnp.concatenate(highs, axis=1), jnp.concatenate(lows, axis=1)], axis=0)
-        return lax.dot_general(feature, both, contract, preferred_element_type=jnp.float32)
+    def product(upper, lower, feature):
+        parts = []
+        for values in (upper, lower):
+            highs = [value.astype(jnp.bfloat16) for value in values]
+            lows = [(value - high.astype(jnp.float32)).astype(jnp.bfloat16) for value, high in zip(values, highs)]
+            parts += [jnp.concatenate(highs, axis=1), jnp.concatenate(lows, axis=1)]
+        return lax.dot_general(feature, jnp.concatenate(parts, axis=0), contract, preferred_element_type=jnp.float32)
 
     def ahead(chunk, slot):
         spans = [chunk * width + j for j in range(width)]
-        coordinate = jnp.concatenate([coordinate_ref[pl.ds(tile, 16, stride=tiles), :].astype(jnp.bfloat16) for tile in spans], axis=1)
+        coordinate = jnp.concatenate([coordinate_ref[pl.ds(tile, 16, stride=pitch), :].astype(jnp.bfloat16) for tile in spans], axis=1)
         flat_ref[slot] = jnp.dot(factors, jnp.concatenate([coordinate] * 3, axis=0), preferred_element_type=jnp.float32)
 
     def one(chunk, slot):
         spans = [chunk * width + j for j in range(width)]
-        feature = jnp.concatenate([feature_ref[pl.ds(tile, 32, stride=tiles), :].astype(jnp.bfloat16) for tile in spans], axis=1)
+        feature = jnp.concatenate([feature_ref[pl.ds(tile, 32, stride=pitch), :].astype(jnp.bfloat16) for tile in spans], axis=1)
         ahead(jnp.minimum(chunk + 1, steps - 1), 1 - slot)
         source = [[source_ref[pl.ds(k * tiles + tile, 1), :] for k in range(3)] for tile in spans]
-        for t in range(0, targets, block):
-            kernels, pulls = [], []
+        for t in (0, LANES):
+            values = [[], []]
             for j in range(width):
-                known = flat_ref[slot, t : t + block, j * LANES : (j + 1) * LANES]
-                deep = column_ref[2, t : t + block, :] - source[j][2]
-                if t < LANES:
-                    squared = deep * deep + known
-                else:
-                    sep = [column_ref[k, t : t + block, :] - source[j][k] for k in range(2)]
-                    squared = sep[0] * sep[0] + sep[1] * sep[1] + (deep * deep + sigma_sq)
-                inverse = lax.rsqrt(squared)
-                square = inverse * inverse
-                kernel = square * inverse
-                kernels.append(kernel)
-                if t >= LANES:
-                    pulls.append((kernel * square) * known)
-            sum_ref[t // block] = sum_ref[t // block] + product(kernels, feature)
-            if t >= LANES:
-                sum_ref[3] = sum_ref[3] + product(pulls, feature)
+                for u in range(2 if t < LANES else 1):
+                    row = t + u * block
+                    known = flat_ref[slot, row : row + block, j * LANES : (j + 1) * LANES]
+                    deep = column_ref[2, row : row + block, :] - source[j][2]
+                    if t < LANES:
+                        squared = deep * deep + known
+                    else:
+                        sep = [column_ref[k, row : row + block, :] - source[j][k] for k in range(2)]
+                        squared = sep[0] * sep[0] + sep[1] * sep[1] + (deep * deep + sigma_sq)
+                    inverse = lax.rsqrt(squared)
+                    square = inverse * inverse
+                    kernel = square * inverse
+                    values[u].append(kernel)
+                    if t >= LANES:
+                        values[1].append((kernel * square) * known)
+            sum_ref[t // LANES] = sum_ref[t // LANES] + product(values[0], values[1], feature)
 
     def step(index, _):
         for j in range(unroll):
@@ -356,7 +358,8 @@
     lax.fori_loop(0, steps // unroll, step, 0)
 
     def combined(index):
-        parts = sum_ref[index, 0:8] + sum_ref[index, 8:16] + sum_ref[index, 16:24]
+        part = slice(index % 2 * LANES, (index % 2 + 1) * LANES)
+        parts = sum_ref[index // 2, 0:8, part] + sum_ref[index // 2, 8:16, part] + sum_ref[index // 2, 16:24, part]
         return parts + pltpu.roll(parts, block, 1)
 
     lane = lax.broadcasted_iota(jnp.int32, (8, LANES), 1)
@@ -455,6 +458,7 @@
     )(v, d, xa, xb, ya, yb, held(own))
 
     tiles = devices + devices // 2
+    pitch = tiles + 1 - tiles % 2
     particle_rates, blob_velocity = pl.pallas_call(
         functools.partial(pair_kernel, cells=(cells_x, cells_y, cells_z)),
         name="pairs",
@@ -463,11 +467,11 @@
         out_specs=[VMEM, VMEM],
         scratch_shapes=[
             pltpu.VMEM((3 * tiles, LANES), f32),
-            pltpu.VMEM((16 * tiles, LANES), f32),
-            pltpu.VMEM((32 * tiles, LANES), f32),
+            pltpu.VMEM((16 * pitch, LANES), f32),
+            pltpu.VMEM((32 * pitch, LANES), f32),
             pltpu.VMEM((devices, LANES), f32),
             pltpu.VMEM((2, targets, 4 * LANES), f32),
-            pltpu.VMEM((4, 32, LANES), f32),
+            pltpu.VMEM((2, 32, 2 * LANES), f32),
         ],
     )(held(everything), held(own), held(columns), held(factors))
     return (vorticity_next, particle_rates, blob_velocity)

time: 31.7 us -> 31.6 us (level)
  no operation moved by 1% of the time
where the time goes in v3:
time: 31.6 us; the launch traced here: 31.3 us
  starting transfers between devices  14.2 us (45%)
  Pallas kernels  10 us (32%)
  waiting for transfers between devices  5.68 us (18%)
  between operations  1.36 us (4%)
    all_to_all x1, starting transfers between devices, per_device(): lax.all_to_all(block.reshape(-1), everyone, 0, 0, tiled=True)  9.78 us
    all_to_all x1, waiting for transfers between devices, per_device(): lax.all_to_all(block.reshape(-1), everyone, 0, 0, tiled=True)  5.67 us
    pallas_call x1, Pallas kernels, per_device(): pl.pallas_call(functools.partial(pair_kernel, cells=(cells_x, cells_y, ce...  3.52 us
    ppermute x1, starting transfers between devices, per_device(): xa = held(lax.ppermute(xa, 'tgt', partners(x_count, 0)))  3.06 us
    pallas_call x1, Pallas kernels, per_device(): pl.pallas_call(grid_kernel, name='grid', out_shape=(jax.ShapeDtypeStruct(...  2.74 us
    pallas_call x1, Pallas kernels, per_device(): pl.pallas_call(local_kernel, name='local', out_shape=(kept(8, cells_z), k...  1.87 us
    pallas_call x1, Pallas kernels, per_device(): pl.pallas_call(faces_kernel, name='faces', out_shape=(kept(3, cells_y, ce...  1.01 us
    pallas_call x1, Pallas kernels, per_device(): pl.pallas_call(block_kernel, name='block', out_shape=(jax.ShapeDtypeStruc...  0.87 us
  transfers between devices with their start and end apart: 5, of which 1 were waited for; matrix products, arithmetic and copies ran while one was open for 0% of the time, Pallas kernels for 15%

profile of v3, /device:TPU:0, one launch (start us, length us, event | category | flops | bytes accessed | tf_op | source)
XLA Modules:
  0.0 31.3 jit_solution(12060181133231400793)
XLA Ops:
  0.6 1.0 %faces.1 = (f32[3,24,256]{2,1,0:T(8,128)S(1)}, f32[3,24,256]{2,1,0:T(8,128)S(1)}, f32[3,12,256]{2,1,0:T(8,128)S(1)}, f32[3,12,256]{2,1,0:T(8,128)S(1)}) custom-call(f32[3,12,24,256]{3,2,1,0:T(8,128)} %v_ref.5), custom_call_target="tpu_custom_call" | custom-call | tf_op jit(solution)/shard_map/faces/pallas_call | solution.py:417
  1.7 3.1 %collective-permute-start = (f32[3,24,256]{2,1,0:T(8,128)S(1)}, f32[3,24,256]{2,1,0:T(8,128)S(1)}, u32[]{:S(2)}, u32[]{:S(2)}) collective-permute-start(f32[3,24,256]{2,1,0:T(8,128)S(1)} %get-tuple-element.18), channel_id=1, source_target_pairs={{0,4},{8,12},{16,20},{24,28},{4,0},{12,8},{20,16},{28,24},{1,5},{9... | collective-permute-start | bytes 221192 | tf_op jit(solution)/shard_map/ppermute | solution.py:429
  4.7 0.7 %collective-permute-start.1 = (f32[3,24,256]{2,1,0:T(8,128)S(1)}, f32[3,24,256]{2,1,0:T(8,128)S(1)}, u32[]{:S(2)}, u32[]{:S(2)}) collective-permute-start(f32[3,24,256]{2,1,0:T(8,128)S(1)} %get-tuple-element.19), channel_id=1, source_target_pairs={{4,8},{12,16},{20,24},{8,4},{16,12},{24,20},{5,9},{13,17},{21,25},... | collective-permute-start | bytes 221192 | tf_op jit(solution)/shard_map/ppermute | solution.py:430
  5.4 0.1 collective-permute-start.2
  5.5 0.7 %collective-permute-start.3 = (f32[3,12,256]{2,1,0:T(8,128)S(1)}, f32[3,12,256]{2,1,0:T(8,128)S(1)}, u32[]{:S(2)}, u32[]{:S(2)}) collective-permute-start(f32[3,12,256]{2,1,0:T(8,128)S(1)} %get-tuple-element.21), channel_id=1, source_target_pairs={{1,2},{2,1},{5,6},{6,5},{9,10},{10,9},{13,14},{14,13},{17,18},{18,... | collective-permute-start | bytes 110600 | tf_op jit(solution)/shard_map/ppermute | solution.py:432
  6.8 1.9 %local.1 = (f32[8,256]{1,0:T(8,128)S(1)}, f32[2,24,256]{2,1,0:T(8,128)S(1)}, f32[2,12,256]{2,1,0:T(8,128)S(1)}, f32[8,128]{1,0:T(8,128)S(1)}) custom-call(s32[1,1]{1,0:T(1,128)} %bitcast.3.live_ref, f32[3,12,24,256]{3,2,1,0:T(8,128)} %v_ref.5, f32[12,24,256]{2,1,0:T(8,128)} %d_ref.3, s32[12,24,256]{2,1,0:T(8,128)} %c_ref.1, f32[3,64]{1,0:T(4,128)} %position_ref.1, ...), custom_call_target="tpu_custom_call" | custom-call | tf_op jit(solution)/shard_map/local/pallas_call | solution.py:435
  8.6 0.0 collective-permute-done.2.ya_ref
  8.7 0.0 collective-permute-done.3.yb_ref
  8.7 0.0 collective-permute-done.xa_ref
  8.7 0.0 collective-permute-done.1.xb_ref
  8.7 0.9 %block.1 = (f32[288,128]{1,0:T(8,128)}, f32[16,128]{1,0:T(8,128)S(1)}) custom-call(f32[8,256]{1,0:T(8,128)S(1)} %get-tuple-element.22.sums_ref, f32[2,24,256]{2,1,0:T(8,128)S(1)} %get-tuple-element.23.wx_ref, f32[2,12,256]{2,1,0:T(8,128)S(1)} %get-tuple-element.24.wy_ref, f32[8,128]{1,0:T(8,128)S(1)} %get-tuple-element.25.row_ref, ...), custom_call_target="tpu_custom_call" | custom-call | tf_op jit(solution)/shard_map/block/pallas_call | solution.py:442
  9.6 9.8 %all-to-all-start = ((f32[32,1152,1]{1,2,0:T(1,128)}), f32[32,1152,1]{1,2,0:T(1,128)S(1)}, u32[]{:S(2)}, u32[]{:S(2)}) async-start(f32[32,1152,1]{1,2,0:T(1,128)} %bitcast.5), calls=%async_computation | async-start | bytes 294912 | tf_op jit(solution)/shard_map/all_to_all | solution.py:449
  19.4 2.7 %grid.1 = (f32[3,12,24,256]{3,2,1,0:T(8,128)}, f32[3,192,128]{2,1,0:T(8,128)S(1)}, bf16[192,128]{1,0:T(8,128)(2,1)S(1)}) custom-call(f32[3,12,24,256]{3,2,1,0:T(8,128)} %v_ref.5, f32[12,24,256]{2,1,0:T(8,128)} %d_ref.3, f32[3,24,256]{2,1,0:T(8,128)S(1)} %collective-permute-done.xa_ref, f32[3,24,256]{2,1,0:T(8,128)S(1)} %collective-permute-done.1.xb_ref, ...), custom_call_target="tpu_custom_call" | custom-call | tf_op jit(solution)/shard_map/grid/pallas_call | solution.py:452
  22.1 5.7 %all-to-all-done = f32[32,1152,1]{1,2,0:T(1,128)S(1)} async-done(((f32[32,1152,1]{1,2,0:T(1,128)}), f32[32,1152,1]{1,2,0:T(1,128)S(1)}, u32[]{:S(2)}, u32[]{:S(2)}) %all-to-all-start) | async-done | bytes 147488 | tf_op jit(solution)/shard_map/all_to_all | solution.py:449
  27.8 3.5 %pairs.1 = (f32[6,64]{1,0:T(8,128)}, f32[3,128]{1,0:T(4,128)}) custom-call(f32[288,128]{1,0:T(8,128)S(1)} %bitcast.4, f32[16,128]{1,0:T(8,128)S(1)} %get-tuple-element.26.own_ref, f32[3,192,128]{2,1,0:T(8,128)S(1)} %get-tuple-element.29.column_ref, bf16[192,128]{1,0:T(8,128)(2,1)S(1)} %get-tuple-element.30.factor_ref), custom_call_target="tpu_custom_call" | custom-call | tf_op jit(solution)/shard_map/pairs/pallas_call | solution.py:462
Async XLA Ops:
  1.7 7.0 %collective-permute-start = (f32[3,24,256]{2,1,0:T(8,128)S(1)}, f32[3,24,256]{2,1,0:T(8,128)S(1)}, u32[]{:S(2)}, u32[]{:S(2)}) collective-permute-start(f32[3,24,256]{2,1,0:T(8,128)S(1)} %get-tuple-element.18), channel_id=1, source_target_pairs={{0,4},{8,12},{16,20},{24,28},{4,0},{12,8},{20,16},{28,24},{1,5},{9... | collective-permute-start | bytes 221192 | tf_op jit(solution)/shard_map/ppermute | solution.py:429
  4.7 4.0 %collective-permute-start.1 = (f32[3,24,256]{2,1,0:T(8,128)S(1)}, f32[3,24,256]{2,1,0:T(8,128)S(1)}, u32[]{:S(2)}, u32[]{:S(2)}) collective-permute-start(f32[3,24,256]{2,1,0:T(8,128)S(1)} %get-tuple-element.19), channel_id=1, source_target_pairs={{4,8},{12,16},{20,24},{8,4},{16,12},{24,20},{5,9},{13,17},{21,25},... | collective-permute-start | bytes 221192 | tf_op jit(solution)/shard_map/ppermute | solution.py:430
  5.4 3.3 %collective-permute-start.2 = (f32[3,12,256]{2,1,0:T(8,128)S(1)}, f32[3,12,256]{2,1,0:T(8,128)S(1)}, u32[]{:S(2)}, u32[]{:S(2)}) collective-permute-start(f32[3,12,256]{2,1,0:T(8,128)S(1)} %get-tuple-element.20), channel_id=1, source_target_pairs={{0,1},{2,3},{1,0},{3,2},{4,5},{6,7},{5,4},{7,6},{8,9},{10,11},{9,8... | collective-permute-start | bytes 110600 | tf_op jit(solution)/shard_map/ppermute | solution.py:431
  5.5 3.2 %collective-permute-start.3 = (f32[3,12,256]{2,1,0:T(8,128)S(1)}, f32[3,12,256]{2,1,0:T(8,128)S(1)}, u32[]{:S(2)}, u32[]{:S(2)}) collective-permute-start(f32[3,12,256]{2,1,0:T(8,128)S(1)} %get-tuple-element.21), channel_id=1, source_target_pairs={{1,2},{2,1},{5,6},{6,5},{9,10},{10,9},{13,14},{14,13},{17,18},{18,... | collective-permute-start | bytes 110600 | tf_op jit(solution)/shard_map/ppermute | solution.py:432
  9.6 18.2 %all-to-all-start = ((f32[32,1152,1]{1,2,0:T(1,128)}), f32[32,1152,1]{1,2,0:T(1,128)S(1)}, u32[]{:S(2)}, u32[]{:S(2)}) async-start(f32[32,1152,1]{1,2,0:T(1,128)} %bitcast.5), calls=%async_computation | async-start | bytes 294912 | tf_op jit(solution)/shard_map/all_to_all | solution.py:449

commit v4 on v3

--- a/solution.py
+++ b/solution.py
@@ -69,29 +69,56 @@
     ]
 
 
-def faces_kernel(v_ref, xa_ref, xb_ref, ya_ref, yb_ref, low_ref, high_ref, sems):
+def crossing(y_index):
+    return lax.rem((y_index + 1) // 2, 2) == 1
+
+
+def faces_kernel(v_ref, xb_ref, ya_ref, second_ref, third_ref, x_ref, low_ref, high_ref, sems):
     _, cells_x, cells_y, _ = v_ref.shape
     x_index, y_index = here()
     x_even = lax.rem(x_index, 2) == 0
     y_even = lax.rem(y_index, 2) == 0
+    y_second = crossing(y_index)
     last = cells_x - 1
     copies = [
-        pltpu.make_async_copy(v_ref.at[:, jnp.where(x_even, 0, last)], xb_ref, sems.at[0]),
-        pltpu.make_async_copy(v_ref.at[:, jnp.where(x_even, last, 0)], xa_ref, sems.at[1]),
-        pltpu.make_async_copy(v_ref.at[:, :, 0:1], low_ref, sems.at[2]),
-        pltpu.make_async_copy(v_ref.at[:, :, cells_y - 1 : cells_y], high_ref, sems.at[3]),
+        pltpu.make_async_copy(v_ref.at[:, :, 0:1], low_ref, sems.at[0]),
+        pltpu.make_async_copy(v_ref.at[:, :, cells_y - 1 : cells_y], high_ref, sems.at[1]),
+        pltpu.make_async_copy(v_ref.at[:, jnp.where(x_even, last, 0)], x_ref, sems.at[2]),
+        pltpu.make_async_copy(v_ref.at[:, jnp.where(x_even, 0, last)], xb_ref, sems.at[3]),
     ]
-    for copy in copies[2:] + copies[:2]:
+    for copy in copies:
         copy.start()
-    copies[2].wait()
-    copies[3].wait()
+    for copy in copies[:3]:
+        copy.wait()
     for k in range(3):
         first = low_ref[k, :, 0, :]
         final = high_ref[k, :, 0, :]
         ya_ref[k] = jnp.where(y_even, final, first)
-        yb_ref[k] = jnp.where(y_even, first, final)
-    copies[0].wait()
-    copies[1].wait()
+        y_face = jnp.where(y_even, first, final)
+        second_ref[k, 0:cells_y] = x_ref[k]
+        third_ref[k, 0:cells_y] = x_ref[k]
+
+        @pl.when(y_second)
+        def _():
+            second_ref[k, 0:cells_x] = y_face
+
+        @pl.when(jnp.logical_not(y_second))
+        def _():
+            third_ref[k, 0:cells_x] = y_face
+
+    copies[3].wait()
+
+
+def layers(k, cells, xb_ref, ya_ref, second_ref, third_ref):
+    cells_x, cells_y = cells
+    x_index, y_index = here()
+    x_even = lax.rem(x_index, 2) == 0
+    y_even = lax.rem(y_index, 2) == 0
+    y_second = crossing(y_index)
+    xa = jnp.where(y_second, third_ref[k, 0:cells_y], second_ref[k, 0:cells_y])
+    yb = jnp.where(y_second, second_ref[k, 0:cells_x], third_ref[k, 0:cells_x])
+    xb, ya = xb_ref[k], ya_ref[k]
+    return jnp.where(x_even, xb, xa), jnp.where(x_even, xa, xb), jnp.where(y_even, yb, ya), jnp.where(y_even, ya, yb)
 
 
 def local_kernel(live_ref, v_ref, d_ref, c_ref, position_ref, strength_ref, sums_ref, wx_ref, wy_ref, row_ref):
@@ -169,20 +196,14 @@
         row_ref[3 + k : 4 + k, :] = jnp.concatenate(parts[2 * k : 2 * k + 2], axis=1)
 
 
-def block_kernel(sums_ref, wx_ref, wy_ref, row_ref, xa_ref, xb_ref, ya_ref, yb_ref, out_ref, own_ref):
-    x_index, y_index = here()
-    x_even = lax.rem(x_index, 2) == 0
-    y_even = lax.rem(y_index, 2) == 0
+def block_kernel(sums_ref, wx_ref, wy_ref, row_ref, xb_ref, ya_ref, second_ref, third_ref, out_ref, own_ref):
     total = sums_ref[...]
+    cells = (wy_ref.shape[1], wx_ref.shape[1])
     rows = []
     for k in range(3):
-        first = jnp.where(x_even, xb_ref[k], xa_ref[k])
-        last = jnp.where(x_even, xa_ref[k], xb_ref[k])
-        row = jnp.sum(wx_ref[0] * first + wx_ref[1] * last, axis=0, keepdims=True)
-        first = jnp.where(y_even, yb_ref[k], ya_ref[k])
-        last = jnp.where(y_even, ya_ref[k], yb_ref[k])
-        row = row + jnp.sum(wy_ref[0] * first + wy_ref[1] * last, axis=0, keepdims=True)
-        rows.append(row)
+        before, beyond, first, last = layers(k, cells, xb_ref, ya_ref, second_ref, third_ref)
+        row = jnp.sum(wx_ref[0] * before + wx_ref[1] * beyond, axis=0, keepdims=True)
+        rows.append(row + jnp.sum(wy_ref[0] * first + wy_ref[1] * last, axis=0, keepdims=True))
     total = total + jnp.concatenate(rows + [jnp.zeros((5, total.shape[1]), jnp.float32)], axis=0)
     strength = seed_weight * pair_lanes(total)
     block = jnp.concatenate([row_ref[0:3], strength[0:3], row_ref[3:6]], axis=0)
@@ -202,17 +223,11 @@
     return rows
 
 
-def grid_kernel(v_ref, d_ref, xa_ref, xb_ref, ya_ref, yb_ref, own_ref, out_ref, column_ref, factor_ref):
+def grid_kernel(v_ref, d_ref, xb_ref, ya_ref, second_ref, third_ref, own_ref, out_ref, column_ref, factor_ref):
     _, cells_x, cells_y, cells_z = v_ref.shape
-    x_index, y_index = here()
-    x_even = lax.rem(x_index, 2) == 0
-    y_even = lax.rem(y_index, 2) == 0
     rows = lax.broadcasted_iota(jnp.int32, (cells_y, cells_z), 0)
     for k in range(3):
-        before = jnp.where(x_even, xb_ref[k], xa_ref[k])
-        beyond = jnp.where(x_even, xa_ref[k], xb_ref[k])
-        first = jnp.where(y_even, yb_ref[k], ya_ref[k])
-        last = jnp.where(y_even, ya_ref[k], yb_ref[k])
+        before, beyond, first, last = layers(k, (cells_x, cells_y), xb_ref, ya_ref, second_ref, third_ref)
         for x in range(cells_x):
             v = v_ref[k, x]
             low = before if x == 0 else v_ref[k, x - 1]
@@ -414,22 +429,32 @@
     def held(array):
         return pltpu.with_memory_space_constraint(array, pltpu.VMEM)
 
-    xa, xb, ya, yb = pl.pallas_call(
+    def number(x, y):
+        return x * y_count + y
+
+    second, third = [], []
+    for y in range(y_count):
+        crossed, straight = (second, third) if (y + 1) // 2 % 2 == 1 else (third, second)
+        straight += [(number(i, y), number(j, y)) for i, j in partners(x_count, 0)]
+        crossed += [(number(x, i), number(x, j)) for i, j in partners(y_count, 1) for x in range(x_count) if i == y]
+    tall = max(cells_x, cells_y)
+    xb, ya, two, three = pl.pallas_call(
         faces_kernel,
         name="faces",
-        out_shape=(kept(3, cells_y, cells_z), kept(3, cells_y, cells_z), kept(3, cells_x, cells_z), kept(3, cells_x, cells_z)),
+        out_shape=(kept(3, cells_y, cells_z), kept(3, cells_x, cells_z), kept(3, tall, cells_z), kept(3, tall, cells_z)),
         in_specs=[pl.BlockSpec(memory_space=pl.ANY)],
         out_specs=[VMEM] * 4,
         scratch_shapes=[
+            pltpu.VMEM((3, cells_y, cells_z), f32),
             pltpu.VMEM((3, cells_x, 1, cells_z), f32),
             pltpu.VMEM((3, cells_x, 1, cells_z), f32),
             pltpu.SemaphoreType.DMA((4,)),
         ],
     )(vorticity)
-    xa = held(lax.ppermute(xa, "tgt", partners(x_count, 0)))
     xb = held(lax.ppermute(xb, "tgt", partners(x_count, 1)))
+    two = held(lax.ppermute(two, everyone, second))
+    three = held(lax.ppermute(three, everyone, third))
     ya = held(lax.ppermute(ya, y_axes, partners(y_count, 0)))
-    yb = held(lax.ppermute(yb, y_axes, partners(y_count, 1)))
 
     v, d, c = vorticity, diffusivity, seed_counts
     sums, wx, wy, rows = pl.pallas_call(
@@ -445,7 +470,7 @@
         out_shape=(jax.ShapeDtypeStruct((devices * GROUPS, LANES), f32), kept(16, LANES)),
         in_specs=[VMEM] * 8,
         out_specs=[VMEM] * 2,
-    )(held(sums), held(wx), held(wy), held(rows), xa, xb, ya, yb)
+    )(held(sums), held(wx), held(wy), held(rows), xb, ya, two, three)
     everything = lax.all_to_all(block.reshape(-1), everyone, 0, 0, tiled=True).reshape(devices * GROUPS, LANES)
 
     targets = LANES + slot_count
@@ -455,7 +480,7 @@
         out_shape=(jax.ShapeDtypeStruct(vorticity.shape, f32), kept(3, targets, LANES), pltpu.VMEM((targets, LANES), jnp.bfloat16)),
         in_specs=[VMEM] * 7,
         out_specs=[VMEM] * 3,
-    )(v, d, xa, xb, ya, yb, held(own))
+    )(vorticity, diffusivity, xb, ya, two, three, held(own))
 
     tiles = devices + devices // 2
     pitch = tiles + 1 - tiles % 2

time: 31.6 us -> 30.9 us (0.978)
  starting transfers between devices: 14.2 us -> 13.6 us
    all_to_all x1, starting transfers between devices: 9.78 us -> 3.79 us  [per_device(): lax.all_to_all(block.reshape(-1), everyone, 0, 0, tiled=True)]
    ppermute x2, starting transfers between devices: 3.72 us -> 6.48 us  [the longest x1 5.82 us: per_device(): two = held(lax.ppermute(two, everyone, second))]
    ppermute x1, starting transfers between devices: 0.07 us -> 2.63 us  [per_device(): ya = held(lax.ppermute(ya, y_axes, partners(y_count, 0)))]
where the time goes in v4:
time: 30.9 us; the launch traced here: 30.6 us
  starting transfers between devices  13.6 us (44%)
  Pallas kernels  9.97 us (32%)
  waiting for transfers between devices  5.67 us (18%)
  between operations  1.35 us (4%)
    ppermute x1, starting transfers between devices, per_device(): two = held(lax.ppermute(two, everyone, second))  5.82 us
    all_to_all x1, waiting for transfers between devices, per_device(): lax.all_to_all(block.reshape(-1), everyone, 0, 0, tiled=True)  5.66 us
    all_to_all x1, starting transfers between devices, per_device(): lax.all_to_all(block.reshape(-1), everyone, 0, 0, tiled=True)  3.79 us
    pallas_call x1, Pallas kernels, per_device(): pl.pallas_call(functools.partial(pair_kernel, cells=(cells_x, cells_y, ce...  3.4 us
    pallas_call x1, Pallas kernels, per_device(): pl.pallas_call(grid_kernel, name='grid', out_shape=(jax.ShapeDtypeStruct(...  2.75 us
    ppermute x1, starting transfers between devices, per_device(): ya = held(lax.ppermute(ya, y_axes, partners(y_count, 0)))  2.63 us
    pallas_call x1, Pallas kernels, per_device(): pl.pallas_call(local_kernel, name='local', out_shape=(kept(8, cells_z), k...  1.87 us
    pallas_call x1, Pallas kernels, per_device(): pl.pallas_call(faces_kernel, name='faces', out_shape=(kept(3, cells_y, ce...  1.07 us
  transfers between devices with their start and end apart: 5, of which 1 were waited for; matrix products, arithmetic and copies ran while one was open for 0% of the time, Pallas kernels for 15%

profile of v4, /device:TPU:0, one launch (start us, length us, event | category | flops | bytes accessed | tf_op | source)
XLA Modules:
  0.0 30.6 jit_solution(14936997287983678632)
XLA Ops:
  0.6 1.1 %faces.1 = (f32[3,24,256]{2,1,0:T(8,128)S(1)}, f32[3,12,256]{2,1,0:T(8,128)S(1)}, f32[3,24,256]{2,1,0:T(8,128)S(1)}, f32[3,24,256]{2,1,0:T(8,128)S(1)}) custom-call(f32[3,12,24,256]{3,2,1,0:T(8,128)} %v_ref.5), custom_call_target="tpu_custom_call" | custom-call | tf_op jit(solution)/shard_map/faces/pallas_call | solution.py:441
  1.7 0.7 %collective-permute-start = (f32[3,24,256]{2,1,0:T(8,128)S(1)}, f32[3,24,256]{2,1,0:T(8,128)S(1)}, u32[]{:S(2)}, u32[]{:S(2)}) collective-permute-start(f32[3,24,256]{2,1,0:T(8,128)S(1)} %get-tuple-element.18), channel_id=1, source_target_pairs={{4,8},{12,16},{20,24},{8,4},{16,12},{24,20},{5,9},{13,17},{21,25},... | collective-permute-start | bytes 221192 | tf_op jit(solution)/shard_map/ppermute | solution.py:454
  2.4 5.8 %collective-permute-start.2 = (f32[3,24,256]{2,1,0:T(8,128)S(1)}, f32[3,24,256]{2,1,0:T(8,128)S(1)}, u32[]{:S(2)}, u32[]{:S(2)}) collective-permute-start(f32[3,24,256]{2,1,0:T(8,128)S(1)} %get-tuple-element.20), channel_id=1, source_target_pairs={{0,4},{8,12},{16,20},{24,28},{4,0},{12,8},{20,16},{28,24},{1,2},{5... | collective-permute-start | bytes 221192 | tf_op jit(solution)/shard_map/ppermute | solution.py:455
  8.2 0.7 %collective-permute-start.3 = (f32[3,24,256]{2,1,0:T(8,128)S(1)}, f32[3,24,256]{2,1,0:T(8,128)S(1)}, u32[]{:S(2)}, u32[]{:S(2)}) collective-permute-start(f32[3,24,256]{2,1,0:T(8,128)S(1)} %get-tuple-element.21), channel_id=1, source_target_pairs={{1,5},{9,13},{17,21},{25,29},{5,1},{13,9},{21,17},{29,25},{2,6},{1... | collective-permute-start | bytes 221192 | tf_op jit(solution)/shard_map/ppermute | solution.py:456
  8.9 2.6 %collective-permute-start.1 = (f32[3,12,256]{2,1,0:T(8,128)S(1)}, f32[3,12,256]{2,1,0:T(8,128)S(1)}, u32[]{:S(2)}, u32[]{:S(2)}) collective-permute-start(f32[3,12,256]{2,1,0:T(8,128)S(1)} %get-tuple-element.19), channel_id=1, source_target_pairs={{0,1},{2,3},{1,0},{3,2},{4,5},{6,7},{5,4},{7,6},{8,9},{10,11},{9,8... | collective-permute-start | bytes 110600 | tf_op jit(solution)/shard_map/ppermute | solution.py:457
  12.1 1.9 %local.1 = (f32[8,256]{1,0:T(8,128)S(1)}, f32[2,24,256]{2,1,0:T(8,128)S(1)}, f32[2,12,256]{2,1,0:T(8,128)S(1)}, f32[8,128]{1,0:T(8,128)S(1)}) custom-call(s32[1,1]{1,0:T(1,128)} %bitcast.3.live_ref, f32[3,12,24,256]{3,2,1,0:T(8,128)} %v_ref.5, f32[12,24,256]{2,1,0:T(8,128)} %d_ref.3, s32[12,24,256]{2,1,0:T(8,128)} %c_ref.1, f32[3,64]{1,0:T(4,128)} %position_ref.1, ...), custom_call_target="tpu_custom_call" | custom-call | tf_op jit(solution)/shard_map/local/pallas_call | solution.py:460
  14.0 0.0 collective-permute-done.1.ya_ref
  14.0 0.0 collective-permute-done.xb_ref
  14.0 0.0 collective-permute-done.2.second_ref
  14.1 0.0 collective-permute-done.3.third_ref
  14.1 0.9 %block.1 = (f32[288,128]{1,0:T(8,128)}, f32[16,128]{1,0:T(8,128)S(1)}) custom-call(f32[8,256]{1,0:T(8,128)S(1)} %get-tuple-element.22.sums_ref, f32[2,24,256]{2,1,0:T(8,128)S(1)} %get-tuple-element.23.wx_ref, f32[2,12,256]{2,1,0:T(8,128)S(1)} %get-tuple-element.24.wy_ref, f32[8,128]{1,0:T(8,128)S(1)} %get-tuple-element.25.row_ref, ...), custom_call_target="tpu_custom_call" | custom-call | tf_op jit(solution)/shard_map/block/pallas_call | solution.py:467
  15.0 3.8 %all-to-all-start = ((f32[32,1152,1]{1,2,0:T(1,128)}), f32[32,1152,1]{1,2,0:T(1,128)S(1)}, u32[]{:S(2)}, u32[]{:S(2)}) async-start(f32[32,1152,1]{1,2,0:T(1,128)} %bitcast.5), calls=%async_computation | async-start | bytes 294912 | tf_op jit(solution)/shard_map/all_to_all | solution.py:474
  18.8 2.8 %grid.1 = (f32[3,12,24,256]{3,2,1,0:T(8,128)}, f32[3,192,128]{2,1,0:T(8,128)S(1)}, bf16[192,128]{1,0:T(8,128)(2,1)S(1)}) custom-call(f32[3,12,24,256]{3,2,1,0:T(8,128)} %v_ref.5, f32[12,24,256]{2,1,0:T(8,128)} %d_ref.3, f32[3,24,256]{2,1,0:T(8,128)S(1)} %collective-permute-done.xb_ref, f32[3,12,256]{2,1,0:T(8,128)S(1)} %collective-permute-done.1.ya_ref, ...), custom_call_target="tpu_custom_call" | custom-call | tf_op jit(solution)/shard_map/grid/pallas_call | solution.py:477
  21.5 5.7 %all-to-all-done = f32[32,1152,1]{1,2,0:T(1,128)S(1)} async-done(((f32[32,1152,1]{1,2,0:T(1,128)}), f32[32,1152,1]{1,2,0:T(1,128)S(1)}, u32[]{:S(2)}, u32[]{:S(2)}) %all-to-all-start) | async-done | bytes 147488 | tf_op jit(solution)/shard_map/all_to_all | solution.py:474
  27.2 3.4 %pairs.1 = (f32[6,64]{1,0:T(8,128)}, f32[3,128]{1,0:T(4,128)}) custom-call(f32[288,128]{1,0:T(8,128)S(1)} %bitcast.4, f32[16,128]{1,0:T(8,128)S(1)} %get-tuple-element.26.own_ref, f32[3,192,128]{2,1,0:T(8,128)S(1)} %get-tuple-element.29.column_ref, bf16[192,128]{1,0:T(8,128)(2,1)S(1)} %get-tuple-element.30.factor_ref), custom_call_target="tpu_custom_call" | custom-call | tf_op jit(solution)/shard_map/pairs/pallas_call | solution.py:487
Async XLA Ops:
  1.7 12.3 %collective-permute-start = (f32[3,24,256]{2,1,0:T(8,128)S(1)}, f32[3,24,256]{2,1,0:T(8,128)S(1)}, u32[]{:S(2)}, u32[]{:S(2)}) collective-permute-start(f32[3,24,256]{2,1,0:T(8,128)S(1)} %get-tuple-element.18), channel_id=1, source_target_pairs={{4,8},{12,16},{20,24},{8,4},{16,12},{24,20},{5,9},{13,17},{21,25},... | collective-permute-start | bytes 221192 | tf_op jit(solution)/shard_map/ppermute | solution.py:454
  2.4 11.7 %collective-permute-start.2 = (f32[3,24,256]{2,1,0:T(8,128)S(1)}, f32[3,24,256]{2,1,0:T(8,128)S(1)}, u32[]{:S(2)}, u32[]{:S(2)}) collective-permute-start(f32[3,24,256]{2,1,0:T(8,128)S(1)} %get-tuple-element.20), channel_id=1, source_target_pairs={{0,4},{8,12},{16,20},{24,28},{4,0},{12,8},{20,16},{28,24},{1,2},{5... | collective-permute-start | bytes 221192 | tf_op jit(solution)/shard_map/ppermute | solution.py:455
  8.2 5.9 %collective-permute-start.3 = (f32[3,24,256]{2,1,0:T(8,128)S(1)}, f32[3,24,256]{2,1,0:T(8,128)S(1)}, u32[]{:S(2)}, u32[]{:S(2)}) collective-permute-start(f32[3,24,256]{2,1,0:T(8,128)S(1)} %get-tuple-element.21), channel_id=1, source_target_pairs={{1,5},{9,13},{17,21},{25,29},{5,1},{13,9},{21,17},{29,25},{2,6},{1... | collective-permute-start | bytes 221192 | tf_op jit(solution)/shard_map/ppermute | solution.py:456
  8.9 5.2 %collective-permute-start.1 = (f32[3,12,256]{2,1,0:T(8,128)S(1)}, f32[3,12,256]{2,1,0:T(8,128)S(1)}, u32[]{:S(2)}, u32[]{:S(2)}) collective-permute-start(f32[3,12,256]{2,1,0:T(8,128)S(1)} %get-tuple-element.19), channel_id=1, source_target_pairs={{0,1},{2,3},{1,0},{3,2},{4,5},{6,7},{5,4},{7,6},{8,9},{10,11},{9,8... | collective-permute-start | bytes 110600 | tf_op jit(solution)/shard_map/ppermute | solution.py:457
  15.0 12.2 %all-to-all-start = ((f32[32,1152,1]{1,2,0:T(1,128)}), f32[32,1152,1]{1,2,0:T(1,128)S(1)}, u32[]{:S(2)}, u32[]{:S(2)}) async-start(f32[32,1152,1]{1,2,0:T(1,128)} %bitcast.5), calls=%async_computation | async-start | bytes 294912 | tf_op jit(solution)/shard_map/all_to_all | solution.py:474
